TPU v7x, 128 devices: a whole 4x4x4 slice. The times are simulated.
128 devices in a mesh: row: 16 (over z_lo, y, core), col: 8 (over x, z_hi).
Axes of the slice: x: 4, y: 4, z: 4 (z_hi: 2, z_lo: 2; z = z_hi * 2 + z_lo), core: 2. Of those that a mesh axis runs over, the one named last changes fastest.
Arguments:
- tokens: bfloat16 [2048, 12288], P('row', 'col'), may hold values from -10 to 10
- qkv_weight: bfloat16 [12288, 3, 8192], P('col', None, 'row'), as said below
- out_weight: bfloat16 [8192, 12288], P('row', 'col'), may hold values from -0.0625 to 0.0625
Outputs:
- mixed: bfloat16 [2048, 12288], P('row', 'col')
Inputs may be any that keep to these rules, and one draw needn't show every extreme that they name: `qkv_weight`: entries of magnitude at most 3 / sqrt(12288).
All inputs are finite; a program needn't handle non-finite values.
Results may differ from a plain program's by a relative error of at most 0.0055.
Values may be sent and summed in bfloat16 or wider, within the bound.
No kernel may reach another device: no remote copies, remote signals or barrier semaphores. Data moves between devices by JAX's collectives and lax.ppermute only.
A program may use at most 128 MiB of HBM per device.

v0:
```python
import math

import jax
import jax.numpy as jnp
from jax import lax
from jax.experimental import pallas as pl
from jax.experimental.pallas import tpu as pltpu
from jax.sharding import Mesh, PartitionSpec as P


HD = 128
BLK = 128
HALF = 64
F32 = jnp.float32
BF16 = jnp.bfloat16
CHUNKS = (((0, 0), (1, 0), (0, 1), (0, 3)), ((0, 2), (1, 1), (1, 3), (1, 2)))
BLOCKS = tuple(b for chunk in CHUNKS for b in chunk)
PIECES = ((0, (0, 1)), (1, (0,)), (1, (1,)))


def move(x, axis, n, step):
    return lax.ppermute(x, axis, [(i, (i + step) % n) for i in range(n)])


def swap(x, axis):
    return move(x, axis, 2, 1)


def order_body(at_ref, in_ref, out_ref):
    for h in range(4):
        first = pl.multiple_of(lax.rem(at_ref[0] + h, 4) * HD, HD)
        for s in range(3):
            out_ref[:, (3 * h + s) * HD : (3 * h + s + 1) * HD] = in_ref[s, :, pl.ds(first, HD)]


def heads_first_own(weight, x, steps=6):
    d = weight.shape[1]
    return pl.pallas_call(
        order_body,
        grid_spec=pltpu.PrefetchScalarGridSpec(
            num_scalar_prefetch=1,
            grid=(steps,),
            in_specs=[pl.BlockSpec((3, d // steps, 4 * HD), lambda k, at: (0, k, 0))],
            out_specs=pl.BlockSpec((d // steps, 12 * HD), lambda k, at: (k, 0)),
        ),
        out_shape=jax.ShapeDtypeStruct((d, 12 * HD), weight.dtype),
        name="order",
        compiler_params=pltpu.CompilerParams(vmem_limit_bytes=10 * 2**20),
    )(x, weight)


def copy_body(at_ref, in_ref, out_ref):
    out_ref[...] = in_ref[...]


def rows_first_own(weight, x):
    n = weight.shape[1]
    return pl.pallas_call(
        copy_body,
        grid_spec=pltpu.PrefetchScalarGridSpec(
            num_scalar_prefetch=1,
            grid=(4,),
            in_specs=[pl.BlockSpec((HD, n), lambda h, at: (lax.rem(at[0] + h, 4), 0))],
            out_specs=pl.BlockSpec((HD, n), lambda h, at: (h, 0)),
        ),
        out_shape=jax.ShapeDtypeStruct(weight.shape, weight.dtype),
        name="turn",
        compiler_params=pltpu.CompilerParams(vmem_limit_bytes=8 * 2**20),
    )(x, weight)


def product(lhs, rhs):
    full = jnp.dot(lhs, rhs, preferred_element_type=F32)
    return full, full.astype(BF16)


def row_of(at_ref, dz, dy, dc):
    zl, y, c = at_ref[0], at_ref[1], at_ref[2]
    return lax.rem(zl + dz, 2) * 8 + lax.rem(y + dy, 4) * 2 + lax.rem(c + dc, 2)


def attend_body(at_ref, *refs):
    n = len(PIECES)
    q_refs, k_refs, v_refs = refs[:n], refs[n : 2 * n], refs[2 * n : 3 * n]
    out_refs = refs[3 * n :]
    keys = jnp.concatenate([r[...] for r in k_refs], axis=0)
    values = jnp.concatenate([r[...] for r in v_refs], axis=0)
    lane = lax.broadcasted_iota(jnp.int32, (1, BLK), 1)
    key_pos = jnp.concatenate(
        [row_of(at_ref, dz, dy, dc) * BLK + lane for i, dcs in PIECES for dc in dcs for dz, dy in CHUNKS[i]],
        axis=1,
    )
    rank = lax.broadcasted_iota(jnp.int32, (HALF, 1), 0) + at_ref[3] * HALF
    scale = math.log2(math.e) / math.sqrt(HD)
    for q_ref, (i, dcs) in zip(q_refs, PIECES):
        rows = len(CHUNKS[i]) * HALF
        for place, dc in enumerate(dcs):
            queries = q_ref[place * rows : (place + 1) * rows]
            query_pos = jnp.concatenate([row_of(at_ref, dz, dy, dc) * BLK + rank for dz, dy in CHUNKS[i]], axis=0)
            scores = lax.dot_general(queries, keys, (((1,), (1,)), ((), ())), preferred_element_type=F32)
            scores = jnp.where(query_pos >= key_pos, scores, -1e30)
            top = jnp.max(scores, axis=1, keepdims=True)
            weights = jnp.exp2((scores - top) * scale)
            total = jnp.sum(weights, axis=1, keepdims=True)
            update = jnp.dot(weights.astype(BF16), values, preferred_element_type=F32)
            out_refs[dc][i * rows : (i + 1) * rows] = (update / total).astype(BF16)


def attention(qs, ks, vs, at):
    count = len(BLOCKS) * HALF
    return pl.pallas_call(
        attend_body,
        grid_spec=pltpu.PrefetchScalarGridSpec(
            num_scalar_prefetch=1,
            grid=(1,),
            in_specs=[pl.BlockSpec(a.shape, lambda i, at: (0, 0)) for a in (*qs, *ks, *vs)],
            out_specs=[pl.BlockSpec((count, HD), lambda i, at: (0, 0)) for _ in range(2)],
        ),
        out_shape=[jax.ShapeDtypeStruct((count, HD), BF16) for _ in range(2)],
        name="attend",
        compiler_params=pltpu.CompilerParams(vmem_limit_bytes=24 * 2**20),
    )(at, *qs, *ks, *vs)


def reduce_over_x(own, other):
    (a, a16), (z, z16) = own, other
    w = a.shape[1] // 4
    cut = lambda part, i: part[:, i * w : (i + 1) * w]
    up = move(cut(a16, 2), "x", 4, 1)
    ad = move(cut(a16, 3), "x", 4, -1)
    down = move(cut(z16, 2), "x", 4, -1)
    zu = move(cut(z16, 1), "x", 4, 1)
    mixed = (cut(a, 1) + up.astype(F32)).astype(BF16)
    au = move(mixed, "x", 4, 1)
    mixed = (cut(z, 3) + down.astype(F32)).astype(BF16)
    zd = move(mixed, "x", 4, -1)
    own_sum = cut(a, 0) + au.astype(F32) + ad.astype(F32)
    return own_sum, cut(z, 0) + zu.astype(F32) + zd.astype(F32)


def halves(q, zh):
    parts = q.reshape(-1, 2, HALF, q.shape[-1])
    low, high = parts[:, 0], parts[:, 1]
    own = jnp.where(zh == 0, low, high)
    other = jnp.where(zh == 0, high, low)
    return own.reshape(-1, q.shape[-1]), other.reshape(-1, q.shape[-1])


def reduce_over_zh(summed, zh):
    t = summed.shape[0]
    summed, zh = lax.optimization_barrier((summed, zh))
    own_q, other_q = halves(summed[:, :HD], zh)
    k, v = summed[:, HD : 2 * HD], summed[:, 2 * HD :]
    sent = jnp.concatenate([k, v, other_q]).astype(BF16)
    got = swap(sent, "zh")
    k = (k + got[:t].astype(F32)).astype(BF16)
    v = (v + got[t : 2 * t].astype(F32)).astype(BF16)
    q = (own_q + got[2 * t :].astype(F32)).astype(BF16)
    return q, k, v


def reduce_over_rows(part, rounded):
    block = {b: part[i * HALF : (i + 1) * HALF] for i, b in enumerate(BLOCKS)}
    sent = {b: rounded[i * HALF : (i + 1) * HALF] for i, b in enumerate(BLOCKS)}
    up = move(jnp.concatenate([sent[0, 1], sent[1, 1]]), "y", 4, 1)
    down = move(jnp.concatenate([sent[0, 3], sent[1, 3]]), "y", 4, -1)
    over = swap(sent[1, 2], "zl")
    first = BLOCKS.index((0, 2)) * HALF
    beyond = lax.optimization_barrier(part)[first : first + HALF]
    past = (beyond + over.astype(F32)).astype(BF16)
    far = move(past, "y", 4, 2)
    near = (block[1, 0] + up[HALF:].astype(F32) + down[HALF:].astype(F32)).astype(BF16)
    side = swap(near, "zl")
    near = block[0, 0] + up[:HALF].astype(F32) + down[:HALF].astype(F32)
    return near + far.astype(F32) + side.astype(F32)


def local(tokens, qkv_weight, out_weight):
    zl, y, c, x, zh = (lax.axis_index(a) for a in ("zl", "y", "c", "x", "zh"))
    x_at = x.reshape(1).astype(jnp.int32)
    place = jnp.stack([zl, y, c, zh]).astype(jnp.int32)
    weight = jnp.transpose(qkv_weight, (1, 0, 2))
    w_qkv = heads_first_own(weight, x_at)
    w_own = rows_first_own(out_weight, x_at)
    w_other = swap(w_own, "c")
    w_out = jnp.concatenate([w.reshape(4, HD, -1) for w in (w_own, w_other)], axis=1)
    w_out = w_out.reshape(8 * HD, -1)

    rows = {(0, 0): tokens}
    rows[1, 0] = swap(tokens, "zl")
    for dy in (1, 3, 2):
        rows[0, dy] = move(tokens, "y", 4, -dy)
    for dy in (1, 3):
        rows[1, dy] = move(rows[1, 0], "y", 4, -dy)
    rows[1, 2] = swap(rows[0, 2], "zl")

    qs, ks, vs = [], [], []
    for j, chunk in enumerate(CHUNKS):
        own = [rows[b] for b in chunk]
        other = [swap(rows[dz, dy], "c") for dz, dy in chunk]
        parts = [product(jnp.concatenate(blocks), w_qkv) for blocks in (own, other)]
        first, second = reduce_over_x(*parts)
        for summed in (jnp.concatenate([first, second]),) if j == 0 else (first, second):
            q, k, v = reduce_over_zh(summed, zh)
            qs.append(q)
            ks.append(k)
            vs.append(v)
    mine, theirs = attention(qs, ks, vs, place)

    pair = jnp.concatenate([mine, swap(theirs, "c")], axis=1)
    near = {0: pair}
    far = {0: swap(pair, "zh")}
    for dx in (1, 3, 2):
        near[dx] = move(pair, "x", 4, -dx)
    for dx in (1, 3):
        far[dx] = move(far[0], "x", 4, -dx)
    far[2] = swap(near[2], "zh")
    sums = []
    for side in (near, far):
        both = product(jnp.concatenate([side[i] for i in range(4)], axis=1), w_out)
        sums.append(lax.optimization_barrier(reduce_over_rows(*both)))
    low = jnp.where(zh == 0, sums[0], sums[1])
    high = jnp.where(zh == 0, sums[1], sums[0])
    return (tokens.astype(F32) + jnp.concatenate([low, high])).astype(BF16)


def solution(mesh):
    fine = Mesh(mesh.devices.reshape(2, 4, 2, 4, 2), ("zl", "y", "c", "x", "zh"))
    row, col = ("zl", "y", "c"), ("x", "zh")
    in_specs = (P(row, col), P(col, None, row), P(row, col))
    return jax.shard_map(local, mesh=fine, in_specs=in_specs, out_specs=P(row, col), check_vma=False)
```

profile of v0, /device:TPU:4, one launch (start us, length us, event | category | flops | bytes accessed | tf_op | source)
XLA Modules:
  0.0 192.1 jit_solution(11674384358295308285)
XLA Ops:
  0.0 1.9 collective-permute-start
  1.9 3.2 %collective-permute-start.14 = (bf16[128,1536]{1,0:T(8,128)(2,1)}, bf16[128,1536]{1,0:T(8,128)(2,1)S(1)}, u32[]{:S(2)}, u32[]{:S(2)}) collective-permute-start(bf16[128,1536]{1,0:T(8,128)(2,1)} %param.3), channel_id=1, source_target_pairs={{0,32},{16,48},{32,0},{48,16},{1,33},{17,49},{33,1},{49,17},{2,34}... | collective-permute-start | bytes 1179656 | tf_op jit(solution)/shard_map/ppermute | solution.py:22
  7.1 2.3 %copy-done = bf16[1536,3,512]{2,0,1:T(8,128)(2,1)S(1)} copy-done((bf16[1536,3,512]{2,0,1:T(8,128)(2,1)S(1)}, bf16[1536,3,512]{2,0,1:T(8,128)(2,1)}, u32[]{:S(2)}) %copy-start) | copy-done | bytes 4718616
  11.2 3.0 %collective-permute-start.15 = (bf16[128,1536]{1,0:T(8,128)(2,1)S(1)}, bf16[128,1536]{1,0:T(8,128)(2,1)S(1)}, u32[]{:S(2)}, u32[]{:S(2)}) collective-permute-start(bf16[128,1536]{1,0:T(8,128)(2,1)S(1)} %collective-permute-done), channel_id=1, source_target_pairs={{0,48},{16,0},{32,16},{48,32},{1,49},{17,1},{33,17},{49,33},{2,50}... | collective-permute-start | bytes 1179656 | tf_op jit(solution)/shard_map/ppermute | solution.py:22
  15.7 1.6 collective-permute-start.16
  17.2 7.2 %collective-permute-done.1 = bf16[128,1536]{1,0:T(8,128)(2,1)S(1)} collective-permute-done((bf16[128,1536]{1,0:T(8,128)(2,1)}, bf16[128,1536]{1,0:T(8,128)(2,1)S(1)}, u32[]{:S(2)}, u32[]{:S(2)}) %collective-permute-start.1) | collective-permute-done | bytes 393248 | tf_op jit(solution)/shard_map/ppermute | solution.py:22
  24.6 2.6 %fusion.81 = (bf16[512,1536]{1,0:T(8,128)(2,1)S(1)}, f32[512,1536]{1,0:T(8,128)S(1)}) fusion(bf16[1536,1536]{1,0:T(8,128)(2,1)S(1)} %order.1, bf16[128,1536]{1,0:T(8,128)(2,1)S(1)} %collective-permute-done.2, bf16[128,1536]{1,0:T(8,128)(2,1)S(1)} %collective-permute-done.1, bf16[128,1536]{1,0:T(8,128)(2,1)S(1)} %collective-permute-done, ...), kind=kOutput, calls=%fused_computation.139 | convolution fusion | flops 2422996992 | bytes 11010048 | tf_op jit(solution)/shard_map/dot_general | solution.py:73
  28.5 2.9 %collective-permute-done.15 = bf16[128,1536]{1,0:T(8,128)(2,1)S(1)} collective-permute-done((bf16[128,1536]{1,0:T(8,128)(2,1)S(1)}, bf16[128,1536]{1,0:T(8,128)(2,1)S(1)}, u32[]{:S(2)}, u32[]{:S(2)}) %collective-permute-start.15) | collective-permute-done | bytes 393248 | tf_op jit(solution)/shard_map/ppermute | solution.py:22
  33.1 2.6 %fusion.83 = (bf16[512,1536]{1,0:T(8,128)(2,1)S(1)}, f32[512,1536]{1,0:T(8,128)S(1)}) fusion(bf16[1536,1536]{1,0:T(8,128)(2,1)S(1)} %order.1, bf16[128,1536]{1,0:T(8,128)(2,1)S(1)} %collective-permute-done.17, bf16[128,1536]{1,0:T(8,128)(2,1)S(1)} %collective-permute-done.16, bf16[128,1536]{1,0:T(8,128)(2,1)S(1)} %collective-permute-done.15, ...), kind=kOutput, calls=%fused_computation.141 | convolution fusion | flops 2422996992 | bytes 11010048 | tf_op jit(solution)/shard_map/dot_general | solution.py:73
  36.9 2.6 %fusion.82 = (bf16[512,1536]{1,0:T(8,128)(2,1)S(1)}, f32[512,1536]{1,0:T(8,128)S(1)}) fusion(bf16[1536,1536]{1,0:T(8,128)(2,1)S(1)} %order.1, bf16[128,1536]{1,0:T(8,128)(2,1)S(1)} %collective-permute-done.9, bf16[128,1536]{1,0:T(8,128)(2,1)S(1)} %collective-permute-done.8, bf16[128,1536]{1,0:T(8,128)(2,1)S(1)} %collective-permute-done.7, ...), kind=kOutput, calls=%fused_computation.140 | convolution fusion | flops 2422996992 | bytes 11010048 | tf_op jit(solution)/shard_map/dot_general | solution.py:73
  41.0 1.5 collective-permute-start.18
  44.4 4.2 %fusion.84 = (bf16[512,1536]{1,0:T(8,128)(2,1)S(1)}, f32[512,1536]{1,0:T(8,128)}) fusion(bf16[1536,1536]{1,0:T(8,128)(2,1)S(1)} %order.1, bf16[128,1536]{1,0:T(8,128)(2,1)S(1)} %collective-permute-done.25, bf16[128,1536]{1,0:T(8,128)(2,1)S(1)} %collective-permute-done.24, bf16[128,1536]{1,0:T(8,128)(2,1)S(1)} %collective-permute-done.23, ...), kind=kOutput, calls=%fused_computation.142 | convolution fusion | flops 2422996992 | bytes 11010048 | tf_op jit(solution)/shard_map/dot_general | solution.py:73
  48.6 3.2 %collective-permute-done.18 = bf16[512,384]{1,0:T(8,128)(2,1)S(1)} collective-permute-done((bf16[512,384]{1,0:T(8,128)(2,1)S(1)}, bf16[512,384]{1,0:T(8,128)(2,1)S(1)}, u32[]{:S(2)}, u32[]{:S(2)}) %collective-permute-start.18) | collective-permute-done | bytes 393248 | tf_op jit(solution)/shard_map/ppermute | solution.py:22
  51.8 1.5 collective-permute-start.4
  53.4 15.0 %collective-permute-done.11 = bf16[512,384]{1,0:T(8,128)(2,1)S(1)} collective-permute-done((bf16[512,384]{1,0:T(8,128)(2,1)S(1)}, bf16[512,384]{1,0:T(8,128)(2,1)S(1)}, u32[]{:S(2)}, u32[]{:S(2)}) %collective-permute-start.11) | collective-permute-done | bytes 393248 | tf_op jit(solution)/shard_map/ppermute | solution.py:22
  68.4 2.4 %collective-permute-start.19 = (bf16[512,384]{1,0:T(8,128)(2,1)S(1)}, bf16[512,384]{1,0:T(8,128)(2,1)S(1)}, u32[]{:S(2)}, u32[]{:S(2)}) collective-permute-start(bf16[512,384]{1,0:T(8,128)(2,1)S(1)} %fusion.42), channel_id=1, source_target_pairs={{0,2},{2,4},{4,6},{6,0},{1,3},{3,5},{5,7},{7,1},{8,10},{10,12},{12... | collective-permute-start | bytes 1179656 | tf_op jit(solution)/shard_map/ppermute | solution.py:22
  71.9 2.0 %collective-permute-start.27 = (bf16[512,384]{1,0:T(8,128)(2,1)}, bf16[512,384]{1,0:T(8,128)(2,1)}, u32[]{:S(2)}, u32[]{:S(2)}) collective-permute-start(bf16[512,384]{1,0:T(8,128)(2,1)} %get-tuple-element.34), channel_id=1, source_target_pairs={{0,6},{2,0},{4,2},{6,4},{1,7},{3,1},{5,3},{7,5},{8,14},{10,8},{12,... | collective-permute-start | bytes 1179656 | tf_op jit(solution)/shard_map/ppermute | solution.py:22
  74.2 6.2 %collective-permute-done.19 = bf16[512,384]{1,0:T(8,128)(2,1)S(1)} collective-permute-done((bf16[512,384]{1,0:T(8,128)(2,1)S(1)}, bf16[512,384]{1,0:T(8,128)(2,1)S(1)}, u32[]{:S(2)}, u32[]{:S(2)}) %collective-permute-start.19) | collective-permute-done | bytes 393248 | tf_op jit(solution)/shard_map/ppermute | solution.py:22
  81.9 6.9 %collective-permute-done.10 = bf16[512,384]{1,0:T(8,128)(2,1)S(1)} collective-permute-done((bf16[512,384]{1,0:T(8,128)(2,1)S(1)}, bf16[512,384]{1,0:T(8,128)(2,1)S(1)}, u32[]{:S(2)}, u32[]{:S(2)}) %collective-permute-start.10) | collective-permute-done | bytes 393248 | tf_op jit(solution)/shard_map/ppermute | solution.py:22
  88.8 1.8 collective-permute-done.12
  92.6 2.1 %fusion.40 = bf16[512,384]{1,0:T(8,128)(2,1)} fusion(f32[512,1536]{1,0:T(8,128)} %get-tuple-element.64, bf16[512,384]{1,0:T(8,128)(2,1)} %collective-permute-done.27), kind=kLoop, calls=%fused_computation.43 | loop fusion | flops 589824 | bytes 1572864 | tf_op jit(solution)/shard_map/convert_element_type | solution.py:135
  94.6 1.7 collective-permute-start.28
  96.3 1.7 pad_maximum_fusion.7
  98.0 3.6 %collective-permute-start.21 = (bf16[1280,128]{1,0:T(8,128)(2,1)}, bf16[1280,128]{1,0:T(8,128)(2,1)}, u32[]{:S(2)}, u32[]{:S(2)}) collective-permute-start(bf16[1280,128]{1,0:T(8,128)(2,1)} %pad_maximum_fusion.7), channel_id=1, source_target_pairs={{0,1},{1,0},{2,3},{3,2},{4,5},{5,4},{6,7},{7,6},{8,9},{9,8},{10,11... | collective-permute-start | bytes 983048 | tf_op jit(solution)/shard_map/ppermute | solution.py:22
  102.7 1.8 pad_maximum_fusion.2
  104.5 1.8 fusion.62
  106.3 3.7 %collective-permute-done.21 = bf16[1280,128]{1,0:T(8,128)(2,1)} collective-permute-done((bf16[1280,128]{1,0:T(8,128)(2,1)}, bf16[1280,128]{1,0:T(8,128)(2,1)}, u32[]{:S(2)}, u32[]{:S(2)}) %collective-permute-start.21) | collective-permute-done | bytes 327712 | tf_op jit(solution)/shard_map/ppermute | solution.py:22
  112.1 1.5 fusion.41
  117.4 4.1 %collective-permute-start.29 = (bf16[1280,128]{1,0:T(8,128)(2,1)S(1)}, bf16[1280,128]{1,0:T(8,128)(2,1)S(1)}, u32[]{:S(2)}, u32[]{:S(2)}) collective-permute-start(bf16[1280,128]{1,0:T(8,128)(2,1)S(1)} %pad_maximum_fusion.8), channel_id=1, source_target_pairs={{0,1},{1,0},{2,3},{3,2},{4,5},{5,4},{6,7},{7,6},{8,9},{9,8},{10,11... | collective-permute-start | bytes 983048 | tf_op jit(solution)/shard_map/ppermute | solution.py:22
  122.5 1.6 collective-permute-done.13
  126.2 2.2 %collective-permute-done.29 = bf16[1280,128]{1,0:T(8,128)(2,1)S(1)} collective-permute-done((bf16[1280,128]{1,0:T(8,128)(2,1)S(1)}, bf16[1280,128]{1,0:T(8,128)(2,1)S(1)}, u32[]{:S(2)}, u32[]{:S(2)}) %collective-permute-start.29) | collective-permute-done | bytes 327712 | tf_op jit(solution)/shard_map/ppermute | solution.py:22
  128.5 4.6 %attend.1 = (bf16[512,128]{1,0:T(8,128)(2,1)S(1)}, bf16[512,128]{1,0:T(8,128)(2,1)S(1)}) custom-call(s32[4]{0:T(128)S(1)} %pad_add_fusion.at_ref, bf16[512,128]{1,0:T(8,128)(2,1)S(1)} %fusion.61.refs_0_, bf16[256,128]{1,0:T(8,128)(2,1)S(1)} %fusion.64.refs_1_, bf16[256,128]{1,0:T(8,128)(2,1)S(1)} %fusion.63.refs_2_, ...), custom_call_target="tpu_custom_call" | custom-call | tf_op jit(solution)/shard_map/attend/pallas_call | solution.py:111
  134.6 1.6 collective-permute-start.32
  136.5 1.7 collective-permute-start.33
  138.2 1.6 pad_maximum_fusion
  139.8 2.2 %collective-permute-start.40 = (bf16[512,256]{1,0:T(8,128)(2,1)S(1)}, bf16[512,256]{1,0:T(8,128)(2,1)S(1)}, u32[]{:S(2)}, u32[]{:S(2)}) collective-permute-start(bf16[512,256]{1,0:T(8,128)(2,1)S(1)} %get-tuple-element.54), channel_id=1, source_target_pairs={{0,1},{1,0},{2,3},{3,2},{4,5},{5,4},{6,7},{7,6},{8,9},{9,8},{10,11... | collective-permute-start | bytes 786440 | tf_op jit(solution)/shard_map/ppermute | solution.py:22
  142.1 6.9 %collective-permute-done.31 = bf16[512,256]{1,0:T(8,128)(2,1)S(1)} collective-permute-done((bf16[512,256]{1,0:T(8,128)(2,1)S(1)}, bf16[512,256]{1,0:T(8,128)(2,1)S(1)}, u32[]{:S(2)}, u32[]{:S(2)}) %collective-permute-start.31) | collective-permute-done | bytes 262176 | tf_op jit(solution)/shard_map/ppermute | solution.py:22
  150.2 1.8 fusion.85
  152.2 2.2 %collective-permute-start.35 = (bf16[128,1536]{1,0:T(8,128)(2,1)S(1)}, bf16[128,1536]{1,0:T(8,128)(2,1)S(1)}, u32[]{:S(2)}, u32[]{:S(2)}) collective-permute-start(bf16[128,1536]{1,0:T(8,128)(2,1)S(1)} %pad_maximum_fusion.3), channel_id=1, source_target_pairs={{0,16},{16,32},{32,48},{48,0},{1,17},{17,33},{33,49},{49,1},{2,18}... | collective-permute-start | bytes 1179656 | tf_op jit(solution)/shard_map/ppermute | solution.py:22
  154.4 1.5 collective-permute-start.36
  156.0 3.6 %collective-permute-start.42 = (bf16[512,256]{1,0:T(8,128)(2,1)S(1)}, bf16[512,256]{1,0:T(8,128)(2,1)S(1)}, u32[]{:S(2)}, u32[]{:S(2)}) collective-permute-start(bf16[512,256]{1,0:T(8,128)(2,1)S(1)} %collective-permute-done.32), channel_id=1, source_target_pairs={{0,1},{1,0},{2,3},{3,2},{4,5},{5,4},{6,7},{7,6},{8,9},{9,8},{10,11... | collective-permute-start | bytes 786440 | tf_op jit(solution)/shard_map/ppermute | solution.py:22
  161.7 5.3 %collective-permute-done.41 = bf16[512,256]{1,0:T(8,128)(2,1)S(1)} collective-permute-done((bf16[512,256]{1,0:T(8,128)(2,1)S(1)}, bf16[512,256]{1,0:T(8,128)(2,1)S(1)}, u32[]{:S(2)}, u32[]{:S(2)}) %collective-permute-start.41) | collective-permute-done | bytes 262176 | tf_op jit(solution)/shard_map/ppermute | solution.py:22
  167.0 1.5 collective-permute-start.38
  168.5 1.8 fusion.86
  172.7 2.3 %collective-permute-start.45 = (bf16[128,1536]{1,0:T(8,128)(2,1)S(1)}, bf16[128,1536]{1,0:T(8,128)(2,1)S(1)}, u32[]{:S(2)}, u32[]{:S(2)}) collective-permute-start(bf16[128,1536]{1,0:T(8,128)(2,1)S(1)} %pad_maximum_fusion.6), channel_id=1, source_target_pairs={{0,48},{16,0},{32,16},{48,32},{1,49},{17,1},{33,17},{49,33},{2,50}... | collective-permute-start | bytes 1179656 | tf_op jit(solution)/shard_map/ppermute | solution.py:22
  177.5 2.7 %collective-permute-start.47 = (bf16[64,1536]{1,0:T(8,128)(2,1)S(1)}, bf16[64,1536]{1,0:T(8,128)(2,1)S(1)}, u32[]{:S(2)}, u32[]{:S(2)}) collective-permute-start(bf16[64,1536]{1,0:T(8,128)(2,1)S(1)} %fusion.51), channel_id=1, source_target_pairs={{0,32},{16,48},{32,0},{48,16},{1,33},{17,49},{33,1},{49,17},{2,34}... | collective-permute-start | bytes 589832 | tf_op jit(solution)/shard_map/ppermute | solution.py:22
  180.2 4.3 %collective-permute-done.44 = bf16[128,1536]{1,0:T(8,128)(2,1)S(1)} collective-permute-done((bf16[128,1536]{1,0:T(8,128)(2,1)S(1)}, bf16[128,1536]{1,0:T(8,128)(2,1)S(1)}, u32[]{:S(2)}, u32[]{:S(2)}) %collective-permute-start.44) | collective-permute-done | bytes 393248 | tf_op jit(solution)/shard_map/ppermute | solution.py:22
  186.8 4.3 %collective-permute-done.48 = bf16[64,1536]{1,0:T(8,128)(2,1)S(1)} collective-permute-done((bf16[64,1536]{1,0:T(8,128)(2,1)S(1)}, bf16[64,1536]{1,0:T(8,128)(2,1)S(1)}, u32[]{:S(2)}, u32[]{:S(2)}) %collective-permute-start.48) | collective-permute-done | bytes 196640 | tf_op jit(solution)/shard_map/ppermute | solution.py:22
  (130 shorter events, 41.3 us)
Async XLA Ops:
  0.0 11.2 %collective-permute-start = (bf16[128,1536]{1,0:T(8,128)(2,1)}, bf16[128,1536]{1,0:T(8,128)(2,1)S(1)}, u32[]{:S(2)}, u32[]{:S(2)}) collective-permute-start(bf16[128,1536]{1,0:T(8,128)(2,1)} %param.3), channel_id=1, source_target_pairs={{0,64},{64,0},{1,65},{65,1},{2,66},{66,2},{3,67},{67,3},{4,68},{68... | collective-permute-start | bytes 1179656 | tf_op jit(solution)/shard_map/ppermute | solution.py:22
  1.9 13.7 %collective-permute-start.14 = (bf16[128,1536]{1,0:T(8,128)(2,1)}, bf16[128,1536]{1,0:T(8,128)(2,1)S(1)}, u32[]{:S(2)}, u32[]{:S(2)}) collective-permute-start(bf16[128,1536]{1,0:T(8,128)(2,1)} %param.3), channel_id=1, source_target_pairs={{0,32},{16,48},{32,0},{48,16},{1,33},{17,49},{33,1},{49,17},{2,34}... | collective-permute-start | bytes 1179656 | tf_op jit(solution)/shard_map/ppermute | solution.py:22
  5.1 19.3 %collective-permute-start.1 = (bf16[128,1536]{1,0:T(8,128)(2,1)}, bf16[128,1536]{1,0:T(8,128)(2,1)S(1)}, u32[]{:S(2)}, u32[]{:S(2)}) collective-permute-start(bf16[128,1536]{1,0:T(8,128)(2,1)} %param.3), channel_id=1, source_target_pairs={{0,48},{16,0},{32,16},{48,32},{1,49},{17,1},{33,17},{49,33},{2,50}... | collective-permute-start | bytes 1179656 | tf_op jit(solution)/shard_map/ppermute | solution.py:22
  6.2 18.4 %collective-permute-start.2 = (bf16[128,1536]{1,0:T(8,128)(2,1)}, bf16[128,1536]{1,0:T(8,128)(2,1)S(1)}, u32[]{:S(2)}, u32[]{:S(2)}) collective-permute-start(bf16[128,1536]{1,0:T(8,128)(2,1)} %param.3), channel_id=1, source_target_pairs={{0,16},{16,32},{32,48},{48,0},{1,17},{17,33},{33,49},{49,1},{2,18}... | collective-permute-start | bytes 1179656 | tf_op jit(solution)/shard_map/ppermute | solution.py:22
  7.1 28.6 %collective-permute-start.6 = (bf16[128,1536]{1,0:T(8,128)(2,1)}, bf16[128,1536]{1,0:T(8,128)(2,1)S(1)}, u32[]{:S(2)}, u32[]{:S(2)}) collective-permute-start(bf16[128,1536]{1,0:T(8,128)(2,1)} %param.3), channel_id=1, source_target_pairs={{0,8},{8,0},{1,9},{9,1},{2,10},{10,2},{3,11},{11,3},{4,12},{12,4},... | collective-permute-start | bytes 1179656 | tf_op jit(solution)/shard_map/ppermute | solution.py:22
  11.2 20.2 %collective-permute-start.15 = (bf16[128,1536]{1,0:T(8,128)(2,1)S(1)}, bf16[128,1536]{1,0:T(8,128)(2,1)S(1)}, u32[]{:S(2)}, u32[]{:S(2)}) collective-permute-start(bf16[128,1536]{1,0:T(8,128)(2,1)S(1)} %collective-permute-done), channel_id=1, source_target_pairs={{0,48},{16,0},{32,16},{48,32},{1,49},{17,1},{33,17},{49,33},{2,50}... | collective-permute-start | bytes 1179656 | tf_op jit(solution)/shard_map/ppermute | solution.py:22
  15.7 15.8 %collective-permute-start.16 = (bf16[128,1536]{1,0:T(8,128)(2,1)S(1)}, bf16[128,1536]{1,0:T(8,128)(2,1)S(1)}, u32[]{:S(2)}, u32[]{:S(2)}) collective-permute-start(bf16[128,1536]{1,0:T(8,128)(2,1)S(1)} %collective-permute-done), channel_id=1, source_target_pairs={{0,16},{16,32},{32,48},{48,0},{1,17},{17,33},{33,49},{49,1},{2,18}... | collective-permute-start | bytes 1179656 | tf_op jit(solution)/shard_map/ppermute | solution.py:22
  24.4 8.7 %collective-permute-start.17 = (bf16[128,1536]{1,0:T(8,128)(2,1)S(1)}, bf16[128,1536]{1,0:T(8,128)(2,1)S(1)}, u32[]{:S(2)}, u32[]{:S(2)}) collective-permute-start(bf16[128,1536]{1,0:T(8,128)(2,1)S(1)} %collective-permute-done.14), channel_id=1, source_target_pairs={{0,64},{64,0},{1,65},{65,1},{2,66},{66,2},{3,67},{67,3},{4,68},{68... | collective-permute-start | bytes 1179656 | tf_op jit(solution)/shard_map/ppermute | solution.py:22
  27.3 12.5 %collective-permute-start.3 = (bf16[512,384]{1,0:T(8,128)(2,1)S(1)}, bf16[512,384]{1,0:T(8,128)(2,1)S(1)}, u32[]{:S(2)}, u32[]{:S(2)}) collective-permute-start(bf16[512,384]{1,0:T(8,128)(2,1)S(1)} %get-tuple-element.39), channel_id=1, source_target_pairs={{0,2},{2,4},{4,6},{6,0},{1,3},{3,5},{5,7},{7,1},{8,10},{10,12},{12... | collective-permute-start | bytes 1179656 | tf_op jit(solution)/shard_map/ppermute | solution.py:22
  31.4 4.9 %collective-permute-start.7 = (bf16[128,1536]{1,0:T(8,128)(2,1)S(1)}, bf16[128,1536]{1,0:T(8,128)(2,1)S(1)}, u32[]{:S(2)}, u32[]{:S(2)}) collective-permute-start(bf16[128,1536]{1,0:T(8,128)(2,1)S(1)} %collective-permute-done), channel_id=1, source_target_pairs={{0,8},{8,0},{1,9},{9,1},{2,10},{10,2},{3,11},{11,3},{4,12},{12,4},... | collective-permute-start | bytes 1179656 | tf_op jit(solution)/shard_map/ppermute | solution.py:22
  31.5 5.0 %collective-permute-start.8 = (bf16[128,1536]{1,0:T(8,128)(2,1)}, bf16[128,1536]{1,0:T(8,128)(2,1)S(1)}, u32[]{:S(2)}, u32[]{:S(2)}) collective-permute-start(bf16[128,1536]{1,0:T(8,128)(2,1)} %copy-done.7), channel_id=1, source_target_pairs={{0,8},{8,0},{1,9},{9,1},{2,10},{10,2},{3,11},{11,3},{4,12},{12,4},... | collective-permute-start | bytes 1179656 | tf_op jit(solution)/shard_map/ppermute | solution.py:22
  33.1 3.7 %collective-permute-start.9 = (bf16[128,1536]{1,0:T(8,128)(2,1)S(1)}, bf16[128,1536]{1,0:T(8,128)(2,1)S(1)}, u32[]{:S(2)}, u32[]{:S(2)}) collective-permute-start(bf16[128,1536]{1,0:T(8,128)(2,1)S(1)} %collective-permute-done.2), channel_id=1, source_target_pairs={{0,8},{8,0},{1,9},{9,1},{2,10},{10,2},{3,11},{11,3},{4,12},{12,4},... | collective-permute-start | bytes 1179656 | tf_op jit(solution)/shard_map/ppermute | solution.py:22
  35.7 4.6 %collective-permute-start.22 = (bf16[128,1536]{1,0:T(8,128)(2,1)S(1)}, bf16[128,1536]{1,0:T(8,128)(2,1)S(1)}, u32[]{:S(2)}, u32[]{:S(2)}) collective-permute-start(bf16[128,1536]{1,0:T(8,128)(2,1)S(1)} %collective-permute-done.14), channel_id=1, source_target_pairs={{0,8},{8,0},{1,9},{9,1},{2,10},{10,2},{3,11},{11,3},{4,12},{12,4},... | collective-permute-start | bytes 1179656 | tf_op jit(solution)/shard_map/ppermute | solution.py:22
  36.3 4.7 %collective-permute-start.23 = (bf16[128,1536]{1,0:T(8,128)(2,1)S(1)}, bf16[128,1536]{1,0:T(8,128)(2,1)S(1)}, u32[]{:S(2)}, u32[]{:S(2)}) collective-permute-start(bf16[128,1536]{1,0:T(8,128)(2,1)S(1)} %collective-permute-done.15), channel_id=1, source_target_pairs={{0,8},{8,0},{1,9},{9,1},{2,10},{10,2},{3,11},{11,3},{4,12},{12,4},... | collective-permute-start | bytes 1179656 | tf_op jit(solution)/shard_map/ppermute | solution.py:22
  36.4 6.1 %collective-permute-start.24 = (bf16[128,1536]{1,0:T(8,128)(2,1)S(1)}, bf16[128,1536]{1,0:T(8,128)(2,1)S(1)}, u32[]{:S(2)}, u32[]{:S(2)}) collective-permute-start(bf16[128,1536]{1,0:T(8,128)(2,1)S(1)} %collective-permute-done.16), channel_id=1, source_target_pairs={{0,8},{8,0},{1,9},{9,1},{2,10},{10,2},{3,11},{11,3},{4,12},{12,4},... | collective-permute-start | bytes 1179656 | tf_op jit(solution)/shard_map/ppermute | solution.py:22
  36.8 6.2 %collective-permute-start.25 = (bf16[128,1536]{1,0:T(8,128)(2,1)S(1)}, bf16[128,1536]{1,0:T(8,128)(2,1)S(1)}, u32[]{:S(2)}, u32[]{:S(2)}) collective-permute-start(bf16[128,1536]{1,0:T(8,128)(2,1)S(1)} %collective-permute-done.17), channel_id=1, source_target_pairs={{0,8},{8,0},{1,9},{9,1},{2,10},{10,2},{3,11},{11,3},{4,12},{12,4},... | collective-permute-start | bytes 1179656 | tf_op jit(solution)/shard_map/ppermute | solution.py:22
  39.7 98.5 %collective-permute-start.34 = (bf16[512,1536]{1,0:T(8,128)(2,1)S(1)}, bf16[512,1536]{1,0:T(8,128)(2,1)}, u32[]{:S(2)}, u32[]{:S(2)}) collective-permute-start(bf16[512,1536]{1,0:T(8,128)(2,1)S(1)} %turn.1), channel_id=1, source_target_pairs={{0,8},{8,0},{1,9},{9,1},{2,10},{10,2},{3,11},{11,3},{4,12},{12,4},... | collective-permute-start | bytes 4718600 | tf_op jit(solution)/shard_map/ppermute | solution.py:22
  40.4 31.5 %collective-permute-start.5 = (bf16[512,384]{1,0:T(8,128)(2,1)S(1)}, bf16[512,384]{1,0:T(8,128)(2,1)S(1)}, u32[]{:S(2)}, u32[]{:S(2)}) collective-permute-start(bf16[512,384]{1,0:T(8,128)(2,1)S(1)} %get-tuple-element.40), channel_id=1, source_target_pairs={{0,6},{2,0},{4,2},{6,4},{1,7},{3,1},{5,3},{7,5},{8,14},{10,8},{12,... | collective-permute-start | bytes 1179656 | tf_op jit(solution)/shard_map/ppermute | solution.py:22
  41.0 10.8 %collective-permute-start.18 = (bf16[512,384]{1,0:T(8,128)(2,1)S(1)}, bf16[512,384]{1,0:T(8,128)(2,1)S(1)}, u32[]{:S(2)}, u32[]{:S(2)}) collective-permute-start(bf16[512,384]{1,0:T(8,128)(2,1)S(1)} %get-tuple-element.35), channel_id=1, source_target_pairs={{0,2},{2,4},{4,6},{6,0},{1,3},{3,5},{5,7},{7,1},{8,10},{10,12},{12... | collective-permute-start | bytes 1179656 | tf_op jit(solution)/shard_map/ppermute | solution.py:22
  42.5 31.6 %collective-permute-start.20 = (bf16[512,384]{1,0:T(8,128)(2,1)S(1)}, bf16[512,384]{1,0:T(8,128)(2,1)S(1)}, u32[]{:S(2)}, u32[]{:S(2)}) collective-permute-start(bf16[512,384]{1,0:T(8,128)(2,1)S(1)} %get-tuple-element.36), channel_id=1, source_target_pairs={{0,6},{2,0},{4,2},{6,4},{1,7},{3,1},{5,3},{7,5},{8,14},{10,8},{12,... | collective-permute-start | bytes 1179656 | tf_op jit(solution)/shard_map/ppermute | solution.py:22
  43.0 25.4 %collective-permute-start.11 = (bf16[512,384]{1,0:T(8,128)(2,1)S(1)}, bf16[512,384]{1,0:T(8,128)(2,1)S(1)}, u32[]{:S(2)}, u32[]{:S(2)}) collective-permute-start(bf16[512,384]{1,0:T(8,128)(2,1)S(1)} %get-tuple-element.42), channel_id=1, source_target_pairs={{0,6},{2,0},{4,2},{6,4},{1,7},{3,1},{5,3},{7,5},{8,14},{10,8},{12,... | collective-permute-start | bytes 1179656 | tf_op jit(solution)/shard_map/ppermute | solution.py:22
  51.8 20.1 %collective-permute-start.4 = (bf16[512,384]{1,0:T(8,128)(2,1)S(1)}, bf16[512,384]{1,0:T(8,128)(2,1)S(1)}, u32[]{:S(2)}, u32[]{:S(2)}) collective-permute-start(bf16[512,384]{1,0:T(8,128)(2,1)S(1)} %fusion.46), channel_id=1, source_target_pairs={{0,2},{2,4},{4,6},{6,0},{1,3},{3,5},{5,7},{7,1},{8,10},{10,12},{12... | collective-permute-start | bytes 1179656 | tf_op jit(solution)/shard_map/ppermute | solution.py:22
  68.4 12.0 %collective-permute-start.19 = (bf16[512,384]{1,0:T(8,128)(2,1)S(1)}, bf16[512,384]{1,0:T(8,128)(2,1)S(1)}, u32[]{:S(2)}, u32[]{:S(2)}) collective-permute-start(bf16[512,384]{1,0:T(8,128)(2,1)S(1)} %fusion.42), channel_id=1, source_target_pairs={{0,2},{2,4},{4,6},{6,0},{1,3},{3,5},{5,7},{7,1},{8,10},{10,12},{12... | collective-permute-start | bytes 1179656 | tf_op jit(solution)/shard_map/ppermute | solution.py:22
  71.9 16.9 %collective-permute-start.10 = (bf16[512,384]{1,0:T(8,128)(2,1)S(1)}, bf16[512,384]{1,0:T(8,128)(2,1)S(1)}, u32[]{:S(2)}, u32[]{:S(2)}) collective-permute-start(bf16[512,384]{1,0:T(8,128)(2,1)S(1)} %get-tuple-element.41), channel_id=1, source_target_pairs={{0,2},{2,4},{4,6},{6,0},{1,3},{3,5},{5,7},{7,1},{8,10},{10,12},{12... | collective-permute-start | bytes 1179656 | tf_op jit(solution)/shard_map/ppermute | solution.py:22
  71.9 20.6 %collective-permute-start.27 = (bf16[512,384]{1,0:T(8,128)(2,1)}, bf16[512,384]{1,0:T(8,128)(2,1)}, u32[]{:S(2)}, u32[]{:S(2)}) collective-permute-start(bf16[512,384]{1,0:T(8,128)(2,1)} %get-tuple-element.34), channel_id=1, source_target_pairs={{0,6},{2,0},{4,2},{6,4},{1,7},{3,1},{5,3},{7,5},{8,14},{10,8},{12,... | collective-permute-start | bytes 1179656 | tf_op jit(solution)/shard_map/ppermute | solution.py:22
  74.1 38.0 %collective-permute-start.26 = (bf16[512,384]{1,0:T(8,128)(2,1)}, bf16[512,384]{1,0:T(8,128)(2,1)}, u32[]{:S(2)}, u32[]{:S(2)}) collective-permute-start(bf16[512,384]{1,0:T(8,128)(2,1)} %get-tuple-element.33), channel_id=1, source_target_pairs={{0,2},{2,4},{4,6},{6,0},{1,3},{3,5},{5,7},{7,1},{8,10},{10,12},{12... | collective-permute-start | bytes 1179656 | tf_op jit(solution)/shard_map/ppermute | solution.py:22
  80.4 10.2 %collective-permute-start.12 = (bf16[512,384]{1,0:T(8,128)(2,1)S(1)}, bf16[512,384]{1,0:T(8,128)(2,1)S(1)}, u32[]{:S(2)}, u32[]{:S(2)}) collective-permute-start(bf16[512,384]{1,0:T(8,128)(2,1)S(1)} %fusion.44), channel_id=1, source_target_pairs={{0,6},{2,0},{4,2},{6,4},{1,7},{3,1},{5,3},{7,5},{8,14},{10,8},{12,... | collective-permute-start | bytes 1179656 | tf_op jit(solution)/shard_map/ppermute | solution.py:22
  94.6 17.4 %collective-permute-start.28 = (bf16[512,384]{1,0:T(8,128)(2,1)}, bf16[512,384]{1,0:T(8,128)(2,1)}, u32[]{:S(2)}, u32[]{:S(2)}) collective-permute-start(bf16[512,384]{1,0:T(8,128)(2,1)} %fusion.40), channel_id=1, source_target_pairs={{0,6},{2,0},{4,2},{6,4},{1,7},{3,1},{5,3},{7,5},{8,14},{10,8},{12,... | collective-permute-start | bytes 1179656 | tf_op jit(solution)/shard_map/ppermute | solution.py:22
  98.0 12.0 %collective-permute-start.21 = (bf16[1280,128]{1,0:T(8,128)(2,1)}, bf16[1280,128]{1,0:T(8,128)(2,1)}, u32[]{:S(2)}, u32[]{:S(2)}) collective-permute-start(bf16[1280,128]{1,0:T(8,128)(2,1)} %pad_maximum_fusion.7), channel_id=1, source_target_pairs={{0,1},{1,0},{2,3},{3,2},{4,5},{5,4},{6,7},{7,6},{8,9},{9,8},{10,11... | collective-permute-start | bytes 983048 | tf_op jit(solution)/shard_map/ppermute | solution.py:22
  104.5 19.6 %collective-permute-start.13 = (bf16[2560,128]{1,0:T(8,128)(2,1)}, bf16[2560,128]{1,0:T(8,128)(2,1)}, u32[]{:S(2)}, u32[]{:S(2)}) collective-permute-start(bf16[2560,128]{1,0:T(8,128)(2,1)} %pad_maximum_fusion.2), channel_id=1, source_target_pairs={{0,1},{1,0},{2,3},{3,2},{4,5},{5,4},{6,7},{7,6},{8,9},{9,8},{10,11... | collective-permute-start | bytes 1966088 | tf_op jit(solution)/shard_map/ppermute | solution.py:22
  117.4 11.0 %collective-permute-start.29 = (bf16[1280,128]{1,0:T(8,128)(2,1)S(1)}, bf16[1280,128]{1,0:T(8,128)(2,1)S(1)}, u32[]{:S(2)}, u32[]{:S(2)}) collective-permute-start(bf16[1280,128]{1,0:T(8,128)(2,1)S(1)} %pad_maximum_fusion.8), channel_id=1, source_target_pairs={{0,1},{1,0},{2,3},{3,2},{4,5},{5,4},{6,7},{7,6},{8,9},{9,8},{10,11... | collective-permute-start | bytes 983048 | tf_op jit(solution)/shard_map/ppermute | solution.py:22
  134.6 14.5 %collective-permute-start.32 = (bf16[512,256]{1,0:T(8,128)(2,1)S(1)}, bf16[512,256]{1,0:T(8,128)(2,1)S(1)}, u32[]{:S(2)}, u32[]{:S(2)}) collective-permute-start(bf16[512,256]{1,0:T(8,128)(2,1)S(1)} %get-tuple-element.54), channel_id=1, source_target_pairs={{0,4},{2,6},{4,0},{6,2},{1,5},{3,7},{5,1},{7,3},{8,12},{10,14},{12... | collective-permute-start | bytes 786440 | tf_op jit(solution)/shard_map/ppermute | solution.py:22
  136.2 12.8 %collective-permute-start.31 = (bf16[512,256]{1,0:T(8,128)(2,1)S(1)}, bf16[512,256]{1,0:T(8,128)(2,1)S(1)}, u32[]{:S(2)}, u32[]{:S(2)}) collective-permute-start(bf16[512,256]{1,0:T(8,128)(2,1)S(1)} %get-tuple-element.54), channel_id=1, source_target_pairs={{0,6},{2,0},{4,2},{6,4},{1,7},{3,1},{5,3},{7,5},{8,14},{10,8},{12,... | collective-permute-start | bytes 786440 | tf_op jit(solution)/shard_map/ppermute | solution.py:22
  136.5 13.7 %collective-permute-start.33 = (bf16[512,256]{1,0:T(8,128)(2,1)S(1)}, bf16[512,256]{1,0:T(8,128)(2,1)S(1)}, u32[]{:S(2)}, u32[]{:S(2)}) collective-permute-start(bf16[512,256]{1,0:T(8,128)(2,1)S(1)} %get-tuple-element.54), channel_id=1, source_target_pairs={{0,2},{2,4},{4,6},{6,0},{1,3},{3,5},{5,7},{7,1},{8,10},{10,12},{12... | collective-permute-start | bytes 786440 | tf_op jit(solution)/shard_map/ppermute | solution.py:22
  139.8 19.8 %collective-permute-start.40 = (bf16[512,256]{1,0:T(8,128)(2,1)S(1)}, bf16[512,256]{1,0:T(8,128)(2,1)S(1)}, u32[]{:S(2)}, u32[]{:S(2)}) collective-permute-start(bf16[512,256]{1,0:T(8,128)(2,1)S(1)} %get-tuple-element.54), channel_id=1, source_target_pairs={{0,1},{1,0},{2,3},{3,2},{4,5},{5,4},{6,7},{7,6},{8,9},{9,8},{10,11... | collective-permute-start | bytes 786440 | tf_op jit(solution)/shard_map/ppermute | solution.py:22
  152.1 8.2 %collective-permute-start.37 = (bf16[64,1536]{1,0:T(8,128)(2,1)S(1)}, bf16[64,1536]{1,0:T(8,128)(2,1)S(1)}, u32[]{:S(2)}, u32[]{:S(2)}) collective-permute-start(bf16[64,1536]{1,0:T(8,128)(2,1)S(1)} %get-tuple-element.23), channel_id=1, source_target_pairs={{0,64},{64,0},{1,65},{65,1},{2,66},{66,2},{3,67},{67,3},{4,68},{68... | collective-permute-start | bytes 589832 | tf_op jit(solution)/shard_map/ppermute | solution.py:22
  152.2 20.5 %collective-permute-start.35 = (bf16[128,1536]{1,0:T(8,128)(2,1)S(1)}, bf16[128,1536]{1,0:T(8,128)(2,1)S(1)}, u32[]{:S(2)}, u32[]{:S(2)}) collective-permute-start(bf16[128,1536]{1,0:T(8,128)(2,1)S(1)} %pad_maximum_fusion.3), channel_id=1, source_target_pairs={{0,16},{16,32},{32,48},{48,0},{1,17},{17,33},{33,49},{49,1},{2,18}... | collective-permute-start | bytes 1179656 | tf_op jit(solution)/shard_map/ppermute | solution.py:22
  154.4 20.5 %collective-permute-start.36 = (bf16[128,1536]{1,0:T(8,128)(2,1)S(1)}, bf16[128,1536]{1,0:T(8,128)(2,1)S(1)}, u32[]{:S(2)}, u32[]{:S(2)}) collective-permute-start(bf16[128,1536]{1,0:T(8,128)(2,1)S(1)} %pad_maximum_fusion.4), channel_id=1, source_target_pairs={{0,48},{16,0},{32,16},{48,32},{1,49},{17,1},{33,17},{49,33},{2,50}... | collective-permute-start | bytes 1179656 | tf_op jit(solution)/shard_map/ppermute | solution.py:22
  156.0 12.6 %collective-permute-start.42 = (bf16[512,256]{1,0:T(8,128)(2,1)S(1)}, bf16[512,256]{1,0:T(8,128)(2,1)S(1)}, u32[]{:S(2)}, u32[]{:S(2)}) collective-permute-start(bf16[512,256]{1,0:T(8,128)(2,1)S(1)} %collective-permute-done.32), channel_id=1, source_target_pairs={{0,1},{1,0},{2,3},{3,2},{4,5},{5,4},{6,7},{7,6},{8,9},{9,8},{10,11... | collective-permute-start | bytes 786440 | tf_op jit(solution)/shard_map/ppermute | solution.py:22
  159.6 7.4 %collective-permute-start.41 = (bf16[512,256]{1,0:T(8,128)(2,1)S(1)}, bf16[512,256]{1,0:T(8,128)(2,1)S(1)}, u32[]{:S(2)}, u32[]{:S(2)}) collective-permute-start(bf16[512,256]{1,0:T(8,128)(2,1)S(1)} %collective-permute-done.40), channel_id=1, source_target_pairs={{0,6},{2,0},{4,2},{6,4},{1,7},{3,1},{5,3},{7,5},{8,14},{10,8},{12,... | collective-permute-start | bytes 786440 | tf_op jit(solution)/shard_map/ppermute | solution.py:22
  160.2 8.3 %collective-permute-start.43 = (bf16[512,256]{1,0:T(8,128)(2,1)S(1)}, bf16[512,256]{1,0:T(8,128)(2,1)S(1)}, u32[]{:S(2)}, u32[]{:S(2)}) collective-permute-start(bf16[512,256]{1,0:T(8,128)(2,1)S(1)} %collective-permute-done.40), channel_id=1, source_target_pairs={{0,2},{2,4},{4,6},{6,0},{1,3},{3,5},{5,7},{7,1},{8,10},{10,12},{12... | collective-permute-start | bytes 786440 | tf_op jit(solution)/shard_map/ppermute | solution.py:22
  167.0 19.5 %collective-permute-start.38 = (bf16[64,1536]{1,0:T(8,128)(2,1)S(1)}, bf16[64,1536]{1,0:T(8,128)(2,1)S(1)}, u32[]{:S(2)}, u32[]{:S(2)}) collective-permute-start(bf16[64,1536]{1,0:T(8,128)(2,1)S(1)} %fusion.57), channel_id=1, source_target_pairs={{0,32},{16,48},{32,0},{48,16},{1,33},{17,49},{33,1},{49,17},{2,34}... | collective-permute-start | bytes 589832 | tf_op jit(solution)/shard_map/ppermute | solution.py:22
  170.4 7.0 %collective-permute-start.46 = (bf16[64,1536]{1,0:T(8,128)(2,1)S(1)}, bf16[64,1536]{1,0:T(8,128)(2,1)S(1)}, u32[]{:S(2)}, u32[]{:S(2)}) collective-permute-start(bf16[64,1536]{1,0:T(8,128)(2,1)S(1)} %get-tuple-element.28), channel_id=1, source_target_pairs={{0,64},{64,0},{1,65},{65,1},{2,66},{66,2},{3,67},{67,3},{4,68},{68... | collective-permute-start | bytes 589832 | tf_op jit(solution)/shard_map/ppermute | solution.py:22
  171.5 12.9 %collective-permute-start.44 = (bf16[128,1536]{1,0:T(8,128)(2,1)S(1)}, bf16[128,1536]{1,0:T(8,128)(2,1)S(1)}, u32[]{:S(2)}, u32[]{:S(2)}) collective-permute-start(bf16[128,1536]{1,0:T(8,128)(2,1)S(1)} %pad_maximum_fusion.5), channel_id=1, source_target_pairs={{0,16},{16,32},{32,48},{48,0},{1,17},{17,33},{33,49},{49,1},{2,18}... | collective-permute-start | bytes 1179656 | tf_op jit(solution)/shard_map/ppermute | solution.py:22
  172.7 12.6 %collective-permute-start.45 = (bf16[128,1536]{1,0:T(8,128)(2,1)S(1)}, bf16[128,1536]{1,0:T(8,128)(2,1)S(1)}, u32[]{:S(2)}, u32[]{:S(2)}) collective-permute-start(bf16[128,1536]{1,0:T(8,128)(2,1)S(1)} %pad_maximum_fusion.6), channel_id=1, source_target_pairs={{0,48},{16,0},{32,16},{48,32},{1,49},{17,1},{33,17},{49,33},{2,50}... | collective-permute-start | bytes 1179656 | tf_op jit(solution)/shard_map/ppermute | solution.py:22
  175.0 11.4 %collective-permute-start.39 = (bf16[64,1536]{1,0:T(8,128)(2,1)S(1)}, bf16[64,1536]{1,0:T(8,128)(2,1)S(1)}, u32[]{:S(2)}, u32[]{:S(2)}) collective-permute-start(bf16[64,1536]{1,0:T(8,128)(2,1)S(1)} %fusion.56), channel_id=1, source_target_pairs={{0,64},{64,0},{1,65},{65,1},{2,66},{66,2},{3,67},{67,3},{4,68},{68... | collective-permute-start | bytes 589832 | tf_op jit(solution)/shard_map/ppermute | solution.py:22
  177.5 9.3 %collective-permute-start.47 = (bf16[64,1536]{1,0:T(8,128)(2,1)S(1)}, bf16[64,1536]{1,0:T(8,128)(2,1)S(1)}, u32[]{:S(2)}, u32[]{:S(2)}) collective-permute-start(bf16[64,1536]{1,0:T(8,128)(2,1)S(1)} %fusion.51), channel_id=1, source_target_pairs={{0,32},{16,48},{32,0},{48,16},{1,33},{17,49},{33,1},{49,17},{2,34}... | collective-permute-start | bytes 589832 | tf_op jit(solution)/shard_map/ppermute | solution.py:22
  185.4 5.8 %collective-permute-start.48 = (bf16[64,1536]{1,0:T(8,128)(2,1)S(1)}, bf16[64,1536]{1,0:T(8,128)(2,1)S(1)}, u32[]{:S(2)}, u32[]{:S(2)}) collective-permute-start(bf16[64,1536]{1,0:T(8,128)(2,1)S(1)} %fusion.50), channel_id=1, source_target_pairs={{0,64},{64,0},{1,65},{65,1},{2,66},{66,2},{3,67},{67,3},{4,68},{68... | collective-permute-start | bytes 589832 | tf_op jit(solution)/shard_map/ppermute | solution.py:22
  (9 other events, 61.5 us)
where the time goes:
time: 195 us; the launch traced here: 192 us
  waiting for transfers between devices  78.8 us (40%)
  starting transfers between devices  61.6 us (32%)
  other arithmetic  21.3 us (11%)
  matrix products  15.7 us (8%)
  local copies, waits for them, and re-layouts  8.27 us (4%)
  Pallas kernels  6.03 us (3%)
    ppermute x49, waiting for transfers between devices, move(): return lax.ppermute(x, axis, [(i, (i + step) % n) for i in range(n)])  78.8 us
    ppermute x49, starting transfers between devices, move(): return lax.ppermute(x, axis, [(i, (i + step) % n) for i in range(n)])  61.6 us
    dot_general x6, matrix products, product(): full = jnp.dot(lhs, rhs, preferred_element_type=F32)  15.7 us
    concatenate x3, other arithmetic, reduce_over_zh(): sent = jnp.concatenate([k, v, other_q]).astype(BF16)  4.56 us
    pallas_call x1, Pallas kernels, attention(): pl.pallas_call(attend_body, grid_spec=pltpu.PrefetchScalarGridSpec(num_sc...  4.56 us
  transfers between devices with their start and end apart: 49, of which 22 were waited for; matrix products, arithmetic and copies ran while one was open for 22% of the time, Pallas kernels for 3%

commit v1 on v0

--- a/solution.py
+++ b/solution.py
@@ -152,10 +152,10 @@
     own_q, other_q = halves(summed[:, :HD], zh)
     k, v = summed[:, HD : 2 * HD], summed[:, 2 * HD :]
     sent = jnp.concatenate([k, v, other_q]).astype(BF16)
-    got = swap(sent, "zh")
-    k = (k + got[:t].astype(F32)).astype(BF16)
-    v = (v + got[t : 2 * t].astype(F32)).astype(BF16)
-    q = (own_q + got[2 * t :].astype(F32)).astype(BF16)
+    got = swap(sent, "zh").astype(F32)
+    k = (k + got[:t]).astype(BF16)
+    v = (v + got[t : 2 * t]).astype(BF16)
+    q = (own_q + got[2 * t :]).astype(BF16)
     return q, k, v
 
 
@@ -169,10 +169,10 @@
     beyond = lax.optimization_barrier(part)[first : first + HALF]
     past = (beyond + over.astype(F32)).astype(BF16)
     far = move(past, "y", 4, 2)
-    near = (block[1, 0] + up[HALF:].astype(F32) + down[HALF:].astype(F32)).astype(BF16)
+    up, down = up.astype(F32), down.astype(F32)
+    near = (block[1, 0] + up[HALF:] + down[HALF:]).astype(BF16)
     side = swap(near, "zl")
-    near = block[0, 0] + up[:HALF].astype(F32) + down[:HALF].astype(F32)
-    return near + far.astype(F32) + side.astype(F32)
+    return block[0, 0] + up[:HALF] + down[:HALF] + far.astype(F32) + side.astype(F32)
 
 
 def local(tokens, qkv_weight, out_weight):

time: 195 us -> 195 us (level)
    convert_element_type x8 -> x15, other arithmetic: 4.41 us -> 3 us  [the longest x3 2.23 us: reduce_over_zh(): got = swap(sent, 'zh').astype(F32)]
  transfers between devices with their start and end apart: 49 -> 49, of which waited for: 22 -> 22; matrix products, arithmetic and copies ran while one was open for 22% -> 21% of each run, Pallas kernels for 3% -> 3%
where the time goes in v1:
time: 195 us; the launch traced here: 192 us
  waiting for transfers between devices  80.1 us (41%)
  starting transfers between devices  61.9 us (32%)
  other arithmetic  19.8 us (10%)
  matrix products  15.6 us (8%)
  local copies, waits for them, and re-layouts  8.22 us (4%)
  Pallas kernels  6.03 us (3%)
    ppermute x49, waiting for transfers between devices, move(): return lax.ppermute(x, axis, [(i, (i + step) % n) for i in range(n)])  80.1 us
    ppermute x49, starting transfers between devices, move(): return lax.ppermute(x, axis, [(i, (i + step) % n) for i in range(n)])  61.9 us
    dot_general x6, matrix products, product(): full = jnp.dot(lhs, rhs, preferred_element_type=F32)  15.6 us
    pallas_call x1, Pallas kernels, attention(): pl.pallas_call(attend_body, grid_spec=pltpu.PrefetchScalarGridSpec(num_sc...  4.56 us
    concatenate x3, other arithmetic, reduce_over_zh(): sent = jnp.concatenate([k, v, other_q]).astype(BF16)  4.55 us
  transfers between devices with their start and end apart: 49, of which 22 were waited for; matrix products, arithmetic and copies ran while one was open for 21% of the time, Pallas kernels for 3%

profile of v1, /device:TPU:4, one launch (start us, length us, event | category | flops | bytes accessed | tf_op | source)
XLA Modules:
  0.0 192.2 jit_solution(10338295251361909553)
XLA Ops:
  0.0 1.9 collective-permute-start
  1.9 3.2 %collective-permute-start.14 = (bf16[128,1536]{1,0:T(8,128)(2,1)}, bf16[128,1536]{1,0:T(8,128)(2,1)S(1)}, u32[]{:S(2)}, u32[]{:S(2)}) collective-permute-start(bf16[128,1536]{1,0:T(8,128)(2,1)} %param.3), channel_id=1, source_target_pairs={{0,32},{16,48},{32,0},{48,16},{1,33},{17,49},{33,1},{49,17},{2,34}... | collective-permute-start | bytes 1179656 | tf_op jit(solution)/shard_map/ppermute | solution.py:22
  7.1 2.3 %copy-done = bf16[1536,3,512]{2,0,1:T(8,128)(2,1)S(1)} copy-done((bf16[1536,3,512]{2,0,1:T(8,128)(2,1)S(1)}, bf16[1536,3,512]{2,0,1:T(8,128)(2,1)}, u32[]{:S(2)}) %copy-start) | copy-done | bytes 4718616
  11.2 3.0 %collective-permute-start.15 = (bf16[128,1536]{1,0:T(8,128)(2,1)S(1)}, bf16[128,1536]{1,0:T(8,128)(2,1)S(1)}, u32[]{:S(2)}, u32[]{:S(2)}) collective-permute-start(bf16[128,1536]{1,0:T(8,128)(2,1)S(1)} %collective-permute-done), channel_id=1, source_target_pairs={{0,48},{16,0},{32,16},{48,32},{1,49},{17,1},{33,17},{49,33},{2,50}... | collective-permute-start | bytes 1179656 | tf_op jit(solution)/shard_map/ppermute | solution.py:22
  15.7 1.6 collective-permute-start.16
  17.2 7.2 %collective-permute-done.1 = bf16[128,1536]{1,0:T(8,128)(2,1)S(1)} collective-permute-done((bf16[128,1536]{1,0:T(8,128)(2,1)}, bf16[128,1536]{1,0:T(8,128)(2,1)S(1)}, u32[]{:S(2)}, u32[]{:S(2)}) %collective-permute-start.1) | collective-permute-done | bytes 393248 | tf_op jit(solution)/shard_map/ppermute | solution.py:22
  24.5 2.6 %fusion.83 = (bf16[512,1536]{1,0:T(8,128)(2,1)S(1)}, f32[512,1536]{1,0:T(8,128)S(1)}) fusion(bf16[1536,1536]{1,0:T(8,128)(2,1)S(1)} %order.1, bf16[128,1536]{1,0:T(8,128)(2,1)S(1)} %collective-permute-done.2, bf16[128,1536]{1,0:T(8,128)(2,1)S(1)} %collective-permute-done.1, bf16[128,1536]{1,0:T(8,128)(2,1)S(1)} %collective-permute-done, ...), kind=kOutput, calls=%fused_computation.145 | convolution fusion | flops 2422996992 | bytes 11010048 | tf_op jit(solution)/shard_map/dot_general | solution.py:73
  28.5 2.9 %collective-permute-done.15 = bf16[128,1536]{1,0:T(8,128)(2,1)S(1)} collective-permute-done((bf16[128,1536]{1,0:T(8,128)(2,1)S(1)}, bf16[128,1536]{1,0:T(8,128)(2,1)S(1)}, u32[]{:S(2)}, u32[]{:S(2)}) %collective-permute-start.15) | collective-permute-done | bytes 393248 | tf_op jit(solution)/shard_map/ppermute | solution.py:22
  33.1 2.6 %fusion.85 = (bf16[512,1536]{1,0:T(8,128)(2,1)S(1)}, f32[512,1536]{1,0:T(8,128)S(1)}) fusion(bf16[1536,1536]{1,0:T(8,128)(2,1)S(1)} %order.1, bf16[128,1536]{1,0:T(8,128)(2,1)S(1)} %collective-permute-done.17, bf16[128,1536]{1,0:T(8,128)(2,1)S(1)} %collective-permute-done.16, bf16[128,1536]{1,0:T(8,128)(2,1)S(1)} %collective-permute-done.15, ...), kind=kOutput, calls=%fused_computation.147 | convolution fusion | flops 2422996992 | bytes 11010048 | tf_op jit(solution)/shard_map/dot_general | solution.py:73
  36.9 2.6 %fusion.84 = (bf16[512,1536]{1,0:T(8,128)(2,1)S(1)}, f32[512,1536]{1,0:T(8,128)S(1)}) fusion(bf16[1536,1536]{1,0:T(8,128)(2,1)S(1)} %order.1, bf16[128,1536]{1,0:T(8,128)(2,1)S(1)} %collective-permute-done.9, bf16[128,1536]{1,0:T(8,128)(2,1)S(1)} %collective-permute-done.8, bf16[128,1536]{1,0:T(8,128)(2,1)S(1)} %collective-permute-done.7, ...), kind=kOutput, calls=%fused_computation.146 | convolution fusion | flops 2422996992 | bytes 11010048 | tf_op jit(solution)/shard_map/dot_general | solution.py:73
  40.9 1.5 collective-permute-start.18
  44.3 4.2 %fusion.86 = (bf16[512,1536]{1,0:T(8,128)(2,1)S(1)}, f32[512,1536]{1,0:T(8,128)}) fusion(bf16[1536,1536]{1,0:T(8,128)(2,1)S(1)} %order.1, bf16[128,1536]{1,0:T(8,128)(2,1)S(1)} %collective-permute-done.25, bf16[128,1536]{1,0:T(8,128)(2,1)S(1)} %collective-permute-done.24, bf16[128,1536]{1,0:T(8,128)(2,1)S(1)} %collective-permute-done.23, ...), kind=kOutput, calls=%fused_computation.148 | convolution fusion | flops 2422996992 | bytes 11010048 | tf_op jit(solution)/shard_map/dot_general | solution.py:73
  48.6 3.2 %collective-permute-done.18 = bf16[512,384]{1,0:T(8,128)(2,1)S(1)} collective-permute-done((bf16[512,384]{1,0:T(8,128)(2,1)S(1)}, bf16[512,384]{1,0:T(8,128)(2,1)S(1)}, u32[]{:S(2)}, u32[]{:S(2)}) %collective-permute-start.18) | collective-permute-done | bytes 393248 | tf_op jit(solution)/shard_map/ppermute | solution.py:22
  51.8 1.5 collective-permute-start.4
  53.4 15.0 %collective-permute-done.11 = bf16[512,384]{1,0:T(8,128)(2,1)S(1)} collective-permute-done((bf16[512,384]{1,0:T(8,128)(2,1)S(1)}, bf16[512,384]{1,0:T(8,128)(2,1)S(1)}, u32[]{:S(2)}, u32[]{:S(2)}) %collective-permute-start.11) | collective-permute-done | bytes 393248 | tf_op jit(solution)/shard_map/ppermute | solution.py:22
  68.4 2.4 %collective-permute-start.19 = (bf16[512,384]{1,0:T(8,128)(2,1)S(1)}, bf16[512,384]{1,0:T(8,128)(2,1)S(1)}, u32[]{:S(2)}, u32[]{:S(2)}) collective-permute-start(bf16[512,384]{1,0:T(8,128)(2,1)S(1)} %fusion.42), channel_id=1, source_target_pairs={{0,2},{2,4},{4,6},{6,0},{1,3},{3,5},{5,7},{7,1},{8,10},{10,12},{12... | collective-permute-start | bytes 1179656 | tf_op jit(solution)/shard_map/ppermute | solution.py:22
  71.9 2.0 %collective-permute-start.27 = (bf16[512,384]{1,0:T(8,128)(2,1)}, bf16[512,384]{1,0:T(8,128)(2,1)}, u32[]{:S(2)}, u32[]{:S(2)}) collective-permute-start(bf16[512,384]{1,0:T(8,128)(2,1)} %get-tuple-element.34), channel_id=1, source_target_pairs={{0,6},{2,0},{4,2},{6,4},{1,7},{3,1},{5,3},{7,5},{8,14},{10,8},{12,... | collective-permute-start | bytes 1179656 | tf_op jit(solution)/shard_map/ppermute | solution.py:22
  74.2 6.2 %collective-permute-done.19 = bf16[512,384]{1,0:T(8,128)(2,1)S(1)} collective-permute-done((bf16[512,384]{1,0:T(8,128)(2,1)S(1)}, bf16[512,384]{1,0:T(8,128)(2,1)S(1)}, u32[]{:S(2)}, u32[]{:S(2)}) %collective-permute-start.19) | collective-permute-done | bytes 393248 | tf_op jit(solution)/shard_map/ppermute | solution.py:22
  81.9 6.9 %collective-permute-done.10 = bf16[512,384]{1,0:T(8,128)(2,1)S(1)} collective-permute-done((bf16[512,384]{1,0:T(8,128)(2,1)S(1)}, bf16[512,384]{1,0:T(8,128)(2,1)S(1)}, u32[]{:S(2)}, u32[]{:S(2)}) %collective-permute-start.10) | collective-permute-done | bytes 393248 | tf_op jit(solution)/shard_map/ppermute | solution.py:22
  88.8 1.8 collective-permute-done.12
  92.5 2.1 %fusion.40 = bf16[512,384]{1,0:T(8,128)(2,1)} fusion(f32[512,1536]{1,0:T(8,128)} %get-tuple-element.64, bf16[512,384]{1,0:T(8,128)(2,1)} %collective-permute-done.27), kind=kLoop, calls=%fused_computation.43 | loop fusion | flops 589824 | bytes 1572864 | tf_op jit(solution)/shard_map/convert_element_type | solution.py:135
  94.5 1.7 collective-permute-start.28
  96.2 1.7 pad_maximum_fusion.7
  97.9 3.6 %collective-permute-start.21 = (bf16[1280,128]{1,0:T(8,128)(2,1)}, bf16[1280,128]{1,0:T(8,128)(2,1)}, u32[]{:S(2)}, u32[]{:S(2)}) collective-permute-start(bf16[1280,128]{1,0:T(8,128)(2,1)} %pad_maximum_fusion.7), channel_id=1, source_target_pairs={{0,1},{1,0},{2,3},{3,2},{4,5},{5,4},{6,7},{7,6},{8,9},{9,8},{10,11... | collective-permute-start | bytes 983048 | tf_op jit(solution)/shard_map/ppermute | solution.py:22
  102.7 1.8 pad_maximum_fusion.2
  104.5 1.8 fusion.64
  106.3 3.7 %collective-permute-done.21 = bf16[1280,128]{1,0:T(8,128)(2,1)} collective-permute-done((bf16[1280,128]{1,0:T(8,128)(2,1)}, bf16[1280,128]{1,0:T(8,128)(2,1)}, u32[]{:S(2)}, u32[]{:S(2)}) %collective-permute-start.21) | collective-permute-done | bytes 327712 | tf_op jit(solution)/shard_map/ppermute | solution.py:22
  111.1 1.5 fusion.41
  116.4 4.1 %collective-permute-start.29 = (bf16[1280,128]{1,0:T(8,128)(2,1)S(1)}, bf16[1280,128]{1,0:T(8,128)(2,1)S(1)}, u32[]{:S(2)}, u32[]{:S(2)}) collective-permute-start(bf16[1280,128]{1,0:T(8,128)(2,1)S(1)} %pad_maximum_fusion.8), channel_id=1, source_target_pairs={{0,1},{1,0},{2,3},{3,2},{4,5},{5,4},{6,7},{7,6},{8,9},{9,8},{10,11... | collective-permute-start | bytes 983048 | tf_op jit(solution)/shard_map/ppermute | solution.py:22
  121.4 2.5 %collective-permute-done.13 = bf16[2560,128]{1,0:T(8,128)(2,1)} collective-permute-done((bf16[2560,128]{1,0:T(8,128)(2,1)}, bf16[2560,128]{1,0:T(8,128)(2,1)}, u32[]{:S(2)}, u32[]{:S(2)}) %collective-permute-start.13) | collective-permute-done | bytes 655392 | tf_op jit(solution)/shard_map/ppermute | solution.py:22
  125.3 3.0 %collective-permute-done.29 = bf16[1280,128]{1,0:T(8,128)(2,1)S(1)} collective-permute-done((bf16[1280,128]{1,0:T(8,128)(2,1)S(1)}, bf16[1280,128]{1,0:T(8,128)(2,1)S(1)}, u32[]{:S(2)}, u32[]{:S(2)}) %collective-permute-start.29) | collective-permute-done | bytes 327712 | tf_op jit(solution)/shard_map/ppermute | solution.py:22
  128.5 4.6 %attend.1 = (bf16[512,128]{1,0:T(8,128)(2,1)S(1)}, bf16[512,128]{1,0:T(8,128)(2,1)S(1)}) custom-call(s32[4]{0:T(128)S(1)} %pad_add_fusion.at_ref, bf16[512,128]{1,0:T(8,128)(2,1)S(1)} %fusion.63.refs_0_, bf16[256,128]{1,0:T(8,128)(2,1)S(1)} %fusion.66.refs_1_, bf16[256,128]{1,0:T(8,128)(2,1)S(1)} %fusion.65.refs_2_, ...), custom_call_target="tpu_custom_call" | custom-call | tf_op jit(solution)/shard_map/attend/pallas_call | solution.py:111
  134.6 1.6 collective-permute-start.32
  136.5 1.7 collective-permute-start.33
  138.2 1.6 pad_maximum_fusion
  139.8 2.2 %collective-permute-start.40 = (bf16[512,256]{1,0:T(8,128)(2,1)S(1)}, bf16[512,256]{1,0:T(8,128)(2,1)S(1)}, u32[]{:S(2)}, u32[]{:S(2)}) collective-permute-start(bf16[512,256]{1,0:T(8,128)(2,1)S(1)} %get-tuple-element.54), channel_id=1, source_target_pairs={{0,1},{1,0},{2,3},{3,2},{4,5},{5,4},{6,7},{7,6},{8,9},{9,8},{10,11... | collective-permute-start | bytes 786440 | tf_op jit(solution)/shard_map/ppermute | solution.py:22
  142.0 7.0 %collective-permute-done.31 = bf16[512,256]{1,0:T(8,128)(2,1)S(1)} collective-permute-done((bf16[512,256]{1,0:T(8,128)(2,1)S(1)}, bf16[512,256]{1,0:T(8,128)(2,1)S(1)}, u32[]{:S(2)}, u32[]{:S(2)}) %collective-permute-start.31) | collective-permute-done | bytes 262176 | tf_op jit(solution)/shard_map/ppermute | solution.py:22
  150.1 1.8 fusion.87
  152.2 2.2 %collective-permute-start.35 = (bf16[128,1536]{1,0:T(8,128)(2,1)S(1)}, bf16[128,1536]{1,0:T(8,128)(2,1)S(1)}, u32[]{:S(2)}, u32[]{:S(2)}) collective-permute-start(bf16[128,1536]{1,0:T(8,128)(2,1)S(1)} %pad_maximum_fusion.3), channel_id=1, source_target_pairs={{0,16},{16,32},{32,48},{48,0},{1,17},{17,33},{33,49},{49,1},{2,18}... | collective-permute-start | bytes 1179656 | tf_op jit(solution)/shard_map/ppermute | solution.py:22
  154.4 1.5 collective-permute-start.36
  155.9 3.6 %collective-permute-start.42 = (bf16[512,256]{1,0:T(8,128)(2,1)S(1)}, bf16[512,256]{1,0:T(8,128)(2,1)S(1)}, u32[]{:S(2)}, u32[]{:S(2)}) collective-permute-start(bf16[512,256]{1,0:T(8,128)(2,1)S(1)} %collective-permute-done.32), channel_id=1, source_target_pairs={{0,1},{1,0},{2,3},{3,2},{4,5},{5,4},{6,7},{7,6},{8,9},{9,8},{10,11... | collective-permute-start | bytes 786440 | tf_op jit(solution)/shard_map/ppermute | solution.py:22
  161.6 5.3 %collective-permute-done.41 = bf16[512,256]{1,0:T(8,128)(2,1)S(1)} collective-permute-done((bf16[512,256]{1,0:T(8,128)(2,1)S(1)}, bf16[512,256]{1,0:T(8,128)(2,1)S(1)}, u32[]{:S(2)}, u32[]{:S(2)}) %collective-permute-start.41) | collective-permute-done | bytes 262176 | tf_op jit(solution)/shard_map/ppermute | solution.py:22
  167.0 1.5 collective-permute-start.38
  168.5 1.8 fusion.88
  172.7 2.3 %collective-permute-start.45 = (bf16[128,1536]{1,0:T(8,128)(2,1)S(1)}, bf16[128,1536]{1,0:T(8,128)(2,1)S(1)}, u32[]{:S(2)}, u32[]{:S(2)}) collective-permute-start(bf16[128,1536]{1,0:T(8,128)(2,1)S(1)} %pad_maximum_fusion.6), channel_id=1, source_target_pairs={{0,48},{16,0},{32,16},{48,32},{1,49},{17,1},{33,17},{49,33},{2,50}... | collective-permute-start | bytes 1179656 | tf_op jit(solution)/shard_map/ppermute | solution.py:22
  177.2 3.1 %collective-permute-start.47 = (bf16[64,1536]{1,0:T(8,128)(2,1)S(1)}, bf16[64,1536]{1,0:T(8,128)(2,1)S(1)}, u32[]{:S(2)}, u32[]{:S(2)}) collective-permute-start(bf16[64,1536]{1,0:T(8,128)(2,1)S(1)} %fusion.52), channel_id=1, source_target_pairs={{0,32},{16,48},{32,0},{48,16},{1,33},{17,49},{33,1},{49,17},{2,34}... | collective-permute-start | bytes 589832 | tf_op jit(solution)/shard_map/ppermute | solution.py:22
  180.3 4.1 %collective-permute-done.44 = bf16[128,1536]{1,0:T(8,128)(2,1)S(1)} collective-permute-done((bf16[128,1536]{1,0:T(8,128)(2,1)S(1)}, bf16[128,1536]{1,0:T(8,128)(2,1)S(1)}, u32[]{:S(2)}, u32[]{:S(2)}) %collective-permute-start.44) | collective-permute-done | bytes 393248 | tf_op jit(solution)/shard_map/ppermute | solution.py:22
  186.8 4.4 %collective-permute-done.48 = bf16[64,1536]{1,0:T(8,128)(2,1)S(1)} collective-permute-done((bf16[64,1536]{1,0:T(8,128)(2,1)S(1)}, bf16[64,1536]{1,0:T(8,128)(2,1)S(1)}, u32[]{:S(2)}, u32[]{:S(2)}) %collective-permute-start.48) | collective-permute-done | bytes 196640 | tf_op jit(solution)/shard_map/ppermute | solution.py:22
  (139 shorter events, 39.2 us)
Async XLA Ops:
  0.0 11.2 %collective-permute-start = (bf16[128,1536]{1,0:T(8,128)(2,1)}, bf16[128,1536]{1,0:T(8,128)(2,1)S(1)}, u32[]{:S(2)}, u32[]{:S(2)}) collective-permute-start(bf16[128,1536]{1,0:T(8,128)(2,1)} %param.3), channel_id=1, source_target_pairs={{0,64},{64,0},{1,65},{65,1},{2,66},{66,2},{3,67},{67,3},{4,68},{68... | collective-permute-start | bytes 1179656 | tf_op jit(solution)/shard_map/ppermute | solution.py:22
  1.9 13.7 %collective-permute-start.14 = (bf16[128,1536]{1,0:T(8,128)(2,1)}, bf16[128,1536]{1,0:T(8,128)(2,1)S(1)}, u32[]{:S(2)}, u32[]{:S(2)}) collective-permute-start(bf16[128,1536]{1,0:T(8,128)(2,1)} %param.3), channel_id=1, source_target_pairs={{0,32},{16,48},{32,0},{48,16},{1,33},{17,49},{33,1},{49,17},{2,34}... | collective-permute-start | bytes 1179656 | tf_op jit(solution)/shard_map/ppermute | solution.py:22
  5.1 19.3 %collective-permute-start.1 = (bf16[128,1536]{1,0:T(8,128)(2,1)}, bf16[128,1536]{1,0:T(8,128)(2,1)S(1)}, u32[]{:S(2)}, u32[]{:S(2)}) collective-permute-start(bf16[128,1536]{1,0:T(8,128)(2,1)} %param.3), channel_id=1, source_target_pairs={{0,48},{16,0},{32,16},{48,32},{1,49},{17,1},{33,17},{49,33},{2,50}... | collective-permute-start | bytes 1179656 | tf_op jit(solution)/shard_map/ppermute | solution.py:22
  6.2 18.4 %collective-permute-start.2 = (bf16[128,1536]{1,0:T(8,128)(2,1)}, bf16[128,1536]{1,0:T(8,128)(2,1)S(1)}, u32[]{:S(2)}, u32[]{:S(2)}) collective-permute-start(bf16[128,1536]{1,0:T(8,128)(2,1)} %param.3), channel_id=1, source_target_pairs={{0,16},{16,32},{32,48},{48,0},{1,17},{17,33},{33,49},{49,1},{2,18}... | collective-permute-start | bytes 1179656 | tf_op jit(solution)/shard_map/ppermute | solution.py:22
  7.1 28.6 %collective-permute-start.6 = (bf16[128,1536]{1,0:T(8,128)(2,1)}, bf16[128,1536]{1,0:T(8,128)(2,1)S(1)}, u32[]{:S(2)}, u32[]{:S(2)}) collective-permute-start(bf16[128,1536]{1,0:T(8,128)(2,1)} %param.3), channel_id=1, source_target_pairs={{0,8},{8,0},{1,9},{9,1},{2,10},{10,2},{3,11},{11,3},{4,12},{12,4},... | collective-permute-start | bytes 1179656 | tf_op jit(solution)/shard_map/ppermute | solution.py:22
  11.2 20.2 %collective-permute-start.15 = (bf16[128,1536]{1,0:T(8,128)(2,1)S(1)}, bf16[128,1536]{1,0:T(8,128)(2,1)S(1)}, u32[]{:S(2)}, u32[]{:S(2)}) collective-permute-start(bf16[128,1536]{1,0:T(8,128)(2,1)S(1)} %collective-permute-done), channel_id=1, source_target_pairs={{0,48},{16,0},{32,16},{48,32},{1,49},{17,1},{33,17},{49,33},{2,50}... | collective-permute-start | bytes 1179656 | tf_op jit(solution)/shard_map/ppermute | solution.py:22
  15.7 15.8 %collective-permute-start.16 = (bf16[128,1536]{1,0:T(8,128)(2,1)S(1)}, bf16[128,1536]{1,0:T(8,128)(2,1)S(1)}, u32[]{:S(2)}, u32[]{:S(2)}) collective-permute-start(bf16[128,1536]{1,0:T(8,128)(2,1)S(1)} %collective-permute-done), channel_id=1, source_target_pairs={{0,16},{16,32},{32,48},{48,0},{1,17},{17,33},{33,49},{49,1},{2,18}... | collective-permute-start | bytes 1179656 | tf_op jit(solution)/shard_map/ppermute | solution.py:22
  24.4 8.7 %collective-permute-start.17 = (bf16[128,1536]{1,0:T(8,128)(2,1)S(1)}, bf16[128,1536]{1,0:T(8,128)(2,1)S(1)}, u32[]{:S(2)}, u32[]{:S(2)}) collective-permute-start(bf16[128,1536]{1,0:T(8,128)(2,1)S(1)} %collective-permute-done.14), channel_id=1, source_target_pairs={{0,64},{64,0},{1,65},{65,1},{2,66},{66,2},{3,67},{67,3},{4,68},{68... | collective-permute-start | bytes 1179656 | tf_op jit(solution)/shard_map/ppermute | solution.py:22
  27.2 12.5 %collective-permute-start.3 = (bf16[512,384]{1,0:T(8,128)(2,1)S(1)}, bf16[512,384]{1,0:T(8,128)(2,1)S(1)}, u32[]{:S(2)}, u32[]{:S(2)}) collective-permute-start(bf16[512,384]{1,0:T(8,128)(2,1)S(1)} %get-tuple-element.39), channel_id=1, source_target_pairs={{0,2},{2,4},{4,6},{6,0},{1,3},{3,5},{5,7},{7,1},{8,10},{10,12},{12... | collective-permute-start | bytes 1179656 | tf_op jit(solution)/shard_map/ppermute | solution.py:22
  31.4 4.9 %collective-permute-start.7 = (bf16[128,1536]{1,0:T(8,128)(2,1)S(1)}, bf16[128,1536]{1,0:T(8,128)(2,1)S(1)}, u32[]{:S(2)}, u32[]{:S(2)}) collective-permute-start(bf16[128,1536]{1,0:T(8,128)(2,1)S(1)} %collective-permute-done), channel_id=1, source_target_pairs={{0,8},{8,0},{1,9},{9,1},{2,10},{10,2},{3,11},{11,3},{4,12},{12,4},... | collective-permute-start | bytes 1179656 | tf_op jit(solution)/shard_map/ppermute | solution.py:22
  31.5 5.0 %collective-permute-start.8 = (bf16[128,1536]{1,0:T(8,128)(2,1)S(1)}, bf16[128,1536]{1,0:T(8,128)(2,1)S(1)}, u32[]{:S(2)}, u32[]{:S(2)}) collective-permute-start(bf16[128,1536]{1,0:T(8,128)(2,1)S(1)} %collective-permute-done.1), channel_id=1, source_target_pairs={{0,8},{8,0},{1,9},{9,1},{2,10},{10,2},{3,11},{11,3},{4,12},{12,4},... | collective-permute-start | bytes 1179656 | tf_op jit(solution)/shard_map/ppermute | solution.py:22
  33.1 3.7 %collective-permute-start.9 = (bf16[128,1536]{1,0:T(8,128)(2,1)S(1)}, bf16[128,1536]{1,0:T(8,128)(2,1)S(1)}, u32[]{:S(2)}, u32[]{:S(2)}) collective-permute-start(bf16[128,1536]{1,0:T(8,128)(2,1)S(1)} %collective-permute-done.2), channel_id=1, source_target_pairs={{0,8},{8,0},{1,9},{9,1},{2,10},{10,2},{3,11},{11,3},{4,12},{12,4},... | collective-permute-start | bytes 1179656 | tf_op jit(solution)/shard_map/ppermute | solution.py:22
  35.7 4.6 %collective-permute-start.22 = (bf16[128,1536]{1,0:T(8,128)(2,1)S(1)}, bf16[128,1536]{1,0:T(8,128)(2,1)S(1)}, u32[]{:S(2)}, u32[]{:S(2)}) collective-permute-start(bf16[128,1536]{1,0:T(8,128)(2,1)S(1)} %collective-permute-done.14), channel_id=1, source_target_pairs={{0,8},{8,0},{1,9},{9,1},{2,10},{10,2},{3,11},{11,3},{4,12},{12,4},... | collective-permute-start | bytes 1179656 | tf_op jit(solution)/shard_map/ppermute | solution.py:22
  36.3 4.6 %collective-permute-start.23 = (bf16[128,1536]{1,0:T(8,128)(2,1)S(1)}, bf16[128,1536]{1,0:T(8,128)(2,1)S(1)}, u32[]{:S(2)}, u32[]{:S(2)}) collective-permute-start(bf16[128,1536]{1,0:T(8,128)(2,1)S(1)} %collective-permute-done.15), channel_id=1, source_target_pairs={{0,8},{8,0},{1,9},{9,1},{2,10},{10,2},{3,11},{11,3},{4,12},{12,4},... | collective-permute-start | bytes 1179656 | tf_op jit(solution)/shard_map/ppermute | solution.py:22
  36.4 6.0 %collective-permute-start.24 = (bf16[128,1536]{1,0:T(8,128)(2,1)S(1)}, bf16[128,1536]{1,0:T(8,128)(2,1)S(1)}, u32[]{:S(2)}, u32[]{:S(2)}) collective-permute-start(bf16[128,1536]{1,0:T(8,128)(2,1)S(1)} %collective-permute-done.16), channel_id=1, source_target_pairs={{0,8},{8,0},{1,9},{9,1},{2,10},{10,2},{3,11},{11,3},{4,12},{12,4},... | collective-permute-start | bytes 1179656 | tf_op jit(solution)/shard_map/ppermute | solution.py:22
  36.8 6.2 %collective-permute-start.25 = (bf16[128,1536]{1,0:T(8,128)(2,1)S(1)}, bf16[128,1536]{1,0:T(8,128)(2,1)S(1)}, u32[]{:S(2)}, u32[]{:S(2)}) collective-permute-start(bf16[128,1536]{1,0:T(8,128)(2,1)S(1)} %collective-permute-done.17), channel_id=1, source_target_pairs={{0,8},{8,0},{1,9},{9,1},{2,10},{10,2},{3,11},{11,3},{4,12},{12,4},... | collective-permute-start | bytes 1179656 | tf_op jit(solution)/shard_map/ppermute | solution.py:22
  39.7 98.5 %collective-permute-start.34 = (bf16[512,1536]{1,0:T(8,128)(2,1)S(1)}, bf16[512,1536]{1,0:T(8,128)(2,1)}, u32[]{:S(2)}, u32[]{:S(2)}) collective-permute-start(bf16[512,1536]{1,0:T(8,128)(2,1)S(1)} %turn.1), channel_id=1, source_target_pairs={{0,8},{8,0},{1,9},{9,1},{2,10},{10,2},{3,11},{11,3},{4,12},{12,4},... | collective-permute-start | bytes 4718600 | tf_op jit(solution)/shard_map/ppermute | solution.py:22
  40.3 31.5 %collective-permute-start.5 = (bf16[512,384]{1,0:T(8,128)(2,1)S(1)}, bf16[512,384]{1,0:T(8,128)(2,1)S(1)}, u32[]{:S(2)}, u32[]{:S(2)}) collective-permute-start(bf16[512,384]{1,0:T(8,128)(2,1)S(1)} %get-tuple-element.40), channel_id=1, source_target_pairs={{0,6},{2,0},{4,2},{6,4},{1,7},{3,1},{5,3},{7,5},{8,14},{10,8},{12,... | collective-permute-start | bytes 1179656 | tf_op jit(solution)/shard_map/ppermute | solution.py:22
  40.9 10.8 %collective-permute-start.18 = (bf16[512,384]{1,0:T(8,128)(2,1)S(1)}, bf16[512,384]{1,0:T(8,128)(2,1)S(1)}, u32[]{:S(2)}, u32[]{:S(2)}) collective-permute-start(bf16[512,384]{1,0:T(8,128)(2,1)S(1)} %get-tuple-element.35), channel_id=1, source_target_pairs={{0,2},{2,4},{4,6},{6,0},{1,3},{3,5},{5,7},{7,1},{8,10},{10,12},{12... | collective-permute-start | bytes 1179656 | tf_op jit(solution)/shard_map/ppermute | solution.py:22
  42.4 31.6 %collective-permute-start.20 = (bf16[512,384]{1,0:T(8,128)(2,1)S(1)}, bf16[512,384]{1,0:T(8,128)(2,1)S(1)}, u32[]{:S(2)}, u32[]{:S(2)}) collective-permute-start(bf16[512,384]{1,0:T(8,128)(2,1)S(1)} %get-tuple-element.36), channel_id=1, source_target_pairs={{0,6},{2,0},{4,2},{6,4},{1,7},{3,1},{5,3},{7,5},{8,14},{10,8},{12,... | collective-permute-start | bytes 1179656 | tf_op jit(solution)/shard_map/ppermute | solution.py:22
  43.0 25.4 %collective-permute-start.11 = (bf16[512,384]{1,0:T(8,128)(2,1)S(1)}, bf16[512,384]{1,0:T(8,128)(2,1)S(1)}, u32[]{:S(2)}, u32[]{:S(2)}) collective-permute-start(bf16[512,384]{1,0:T(8,128)(2,1)S(1)} %get-tuple-element.42), channel_id=1, source_target_pairs={{0,6},{2,0},{4,2},{6,4},{1,7},{3,1},{5,3},{7,5},{8,14},{10,8},{12,... | collective-permute-start | bytes 1179656 | tf_op jit(solution)/shard_map/ppermute | solution.py:22
  51.8 20.1 %collective-permute-start.4 = (bf16[512,384]{1,0:T(8,128)(2,1)S(1)}, bf16[512,384]{1,0:T(8,128)(2,1)S(1)}, u32[]{:S(2)}, u32[]{:S(2)}) collective-permute-start(bf16[512,384]{1,0:T(8,128)(2,1)S(1)} %fusion.46), channel_id=1, source_target_pairs={{0,2},{2,4},{4,6},{6,0},{1,3},{3,5},{5,7},{7,1},{8,10},{10,12},{12... | collective-permute-start | bytes 1179656 | tf_op jit(solution)/shard_map/ppermute | solution.py:22
  68.4 12.0 %collective-permute-start.19 = (bf16[512,384]{1,0:T(8,128)(2,1)S(1)}, bf16[512,384]{1,0:T(8,128)(2,1)S(1)}, u32[]{:S(2)}, u32[]{:S(2)}) collective-permute-start(bf16[512,384]{1,0:T(8,128)(2,1)S(1)} %fusion.42), channel_id=1, source_target_pairs={{0,2},{2,4},{4,6},{6,0},{1,3},{3,5},{5,7},{7,1},{8,10},{10,12},{12... | collective-permute-start | bytes 1179656 | tf_op jit(solution)/shard_map/ppermute | solution.py:22
  71.9 16.9 %collective-permute-start.10 = (bf16[512,384]{1,0:T(8,128)(2,1)S(1)}, bf16[512,384]{1,0:T(8,128)(2,1)S(1)}, u32[]{:S(2)}, u32[]{:S(2)}) collective-permute-start(bf16[512,384]{1,0:T(8,128)(2,1)S(1)} %get-tuple-element.41), channel_id=1, source_target_pairs={{0,2},{2,4},{4,6},{6,0},{1,3},{3,5},{5,7},{7,1},{8,10},{10,12},{12... | collective-permute-start | bytes 1179656 | tf_op jit(solution)/shard_map/ppermute | solution.py:22
  71.9 20.6 %collective-permute-start.27 = (bf16[512,384]{1,0:T(8,128)(2,1)}, bf16[512,384]{1,0:T(8,128)(2,1)}, u32[]{:S(2)}, u32[]{:S(2)}) collective-permute-start(bf16[512,384]{1,0:T(8,128)(2,1)} %get-tuple-element.34), channel_id=1, source_target_pairs={{0,6},{2,0},{4,2},{6,4},{1,7},{3,1},{5,3},{7,5},{8,14},{10,8},{12,... | collective-permute-start | bytes 1179656 | tf_op jit(solution)/shard_map/ppermute | solution.py:22
  74.0 37.0 %collective-permute-start.26 = (bf16[512,384]{1,0:T(8,128)(2,1)}, bf16[512,384]{1,0:T(8,128)(2,1)}, u32[]{:S(2)}, u32[]{:S(2)}) collective-permute-start(bf16[512,384]{1,0:T(8,128)(2,1)} %get-tuple-element.33), channel_id=1, source_target_pairs={{0,2},{2,4},{4,6},{6,0},{1,3},{3,5},{5,7},{7,1},{8,10},{10,12},{12... | collective-permute-start | bytes 1179656 | tf_op jit(solution)/shard_map/ppermute | solution.py:22
  80.4 10.2 %collective-permute-start.12 = (bf16[512,384]{1,0:T(8,128)(2,1)S(1)}, bf16[512,384]{1,0:T(8,128)(2,1)S(1)}, u32[]{:S(2)}, u32[]{:S(2)}) collective-permute-start(bf16[512,384]{1,0:T(8,128)(2,1)S(1)} %fusion.44), channel_id=1, source_target_pairs={{0,6},{2,0},{4,2},{6,4},{1,7},{3,1},{5,3},{7,5},{8,14},{10,8},{12,... | collective-permute-start | bytes 1179656 | tf_op jit(solution)/shard_map/ppermute | solution.py:22
  94.5 16.5 %collective-permute-start.28 = (bf16[512,384]{1,0:T(8,128)(2,1)}, bf16[512,384]{1,0:T(8,128)(2,1)}, u32[]{:S(2)}, u32[]{:S(2)}) collective-permute-start(bf16[512,384]{1,0:T(8,128)(2,1)} %fusion.40), channel_id=1, source_target_pairs={{0,6},{2,0},{4,2},{6,4},{1,7},{3,1},{5,3},{7,5},{8,14},{10,8},{12,... | collective-permute-start | bytes 1179656 | tf_op jit(solution)/shard_map/ppermute | solution.py:22
  97.9 12.0 %collective-permute-start.21 = (bf16[1280,128]{1,0:T(8,128)(2,1)}, bf16[1280,128]{1,0:T(8,128)(2,1)}, u32[]{:S(2)}, u32[]{:S(2)}) collective-permute-start(bf16[1280,128]{1,0:T(8,128)(2,1)} %pad_maximum_fusion.7), channel_id=1, source_target_pairs={{0,1},{1,0},{2,3},{3,2},{4,5},{5,4},{6,7},{7,6},{8,9},{9,8},{10,11... | collective-permute-start | bytes 983048 | tf_op jit(solution)/shard_map/ppermute | solution.py:22
  104.5 19.5 %collective-permute-start.13 = (bf16[2560,128]{1,0:T(8,128)(2,1)}, bf16[2560,128]{1,0:T(8,128)(2,1)}, u32[]{:S(2)}, u32[]{:S(2)}) collective-permute-start(bf16[2560,128]{1,0:T(8,128)(2,1)} %pad_maximum_fusion.2), channel_id=1, source_target_pairs={{0,1},{1,0},{2,3},{3,2},{4,5},{5,4},{6,7},{7,6},{8,9},{9,8},{10,11... | collective-permute-start | bytes 1966088 | tf_op jit(solution)/shard_map/ppermute | solution.py:22
  116.4 12.0 %collective-permute-start.29 = (bf16[1280,128]{1,0:T(8,128)(2,1)S(1)}, bf16[1280,128]{1,0:T(8,128)(2,1)S(1)}, u32[]{:S(2)}, u32[]{:S(2)}) collective-permute-start(bf16[1280,128]{1,0:T(8,128)(2,1)S(1)} %pad_maximum_fusion.8), channel_id=1, source_target_pairs={{0,1},{1,0},{2,3},{3,2},{4,5},{5,4},{6,7},{7,6},{8,9},{9,8},{10,11... | collective-permute-start | bytes 983048 | tf_op jit(solution)/shard_map/ppermute | solution.py:22
  134.6 14.5 %collective-permute-start.32 = (bf16[512,256]{1,0:T(8,128)(2,1)S(1)}, bf16[512,256]{1,0:T(8,128)(2,1)S(1)}, u32[]{:S(2)}, u32[]{:S(2)}) collective-permute-start(bf16[512,256]{1,0:T(8,128)(2,1)S(1)} %get-tuple-element.54), channel_id=1, source_target_pairs={{0,4},{2,6},{4,0},{6,2},{1,5},{3,7},{5,1},{7,3},{8,12},{10,14},{12... | collective-permute-start | bytes 786440 | tf_op jit(solution)/shard_map/ppermute | solution.py:22
  136.2 12.8 %collective-permute-start.31 = (bf16[512,256]{1,0:T(8,128)(2,1)S(1)}, bf16[512,256]{1,0:T(8,128)(2,1)S(1)}, u32[]{:S(2)}, u32[]{:S(2)}) collective-permute-start(bf16[512,256]{1,0:T(8,128)(2,1)S(1)} %get-tuple-element.54), channel_id=1, source_target_pairs={{0,6},{2,0},{4,2},{6,4},{1,7},{3,1},{5,3},{7,5},{8,14},{10,8},{12,... | collective-permute-start | bytes 786440 | tf_op jit(solution)/shard_map/ppermute | solution.py:22
  136.5 13.7 %collective-permute-start.33 = (bf16[512,256]{1,0:T(8,128)(2,1)S(1)}, bf16[512,256]{1,0:T(8,128)(2,1)S(1)}, u32[]{:S(2)}, u32[]{:S(2)}) collective-permute-start(bf16[512,256]{1,0:T(8,128)(2,1)S(1)} %get-tuple-element.54), channel_id=1, source_target_pairs={{0,2},{2,4},{4,6},{6,0},{1,3},{3,5},{5,7},{7,1},{8,10},{10,12},{12... | collective-permute-start | bytes 786440 | tf_op jit(solution)/shard_map/ppermute | solution.py:22
  139.8 19.7 %collective-permute-start.40 = (bf16[512,256]{1,0:T(8,128)(2,1)S(1)}, bf16[512,256]{1,0:T(8,128)(2,1)S(1)}, u32[]{:S(2)}, u32[]{:S(2)}) collective-permute-start(bf16[512,256]{1,0:T(8,128)(2,1)S(1)} %get-tuple-element.54), channel_id=1, source_target_pairs={{0,1},{1,0},{2,3},{3,2},{4,5},{5,4},{6,7},{7,6},{8,9},{9,8},{10,11... | collective-permute-start | bytes 786440 | tf_op jit(solution)/shard_map/ppermute | solution.py:22
  152.0 8.2 %collective-permute-start.37 = (bf16[64,1536]{1,0:T(8,128)(2,1)S(1)}, bf16[64,1536]{1,0:T(8,128)(2,1)S(1)}, u32[]{:S(2)}, u32[]{:S(2)}) collective-permute-start(bf16[64,1536]{1,0:T(8,128)(2,1)S(1)} %get-tuple-element.23), channel_id=1, source_target_pairs={{0,64},{64,0},{1,65},{65,1},{2,66},{66,2},{3,67},{67,3},{4,68},{68... | collective-permute-start | bytes 589832 | tf_op jit(solution)/shard_map/ppermute | solution.py:22
  152.2 20.5 %collective-permute-start.35 = (bf16[128,1536]{1,0:T(8,128)(2,1)S(1)}, bf16[128,1536]{1,0:T(8,128)(2,1)S(1)}, u32[]{:S(2)}, u32[]{:S(2)}) collective-permute-start(bf16[128,1536]{1,0:T(8,128)(2,1)S(1)} %pad_maximum_fusion.3), channel_id=1, source_target_pairs={{0,16},{16,32},{32,48},{48,0},{1,17},{17,33},{33,49},{49,1},{2,18}... | collective-permute-start | bytes 1179656 | tf_op jit(solution)/shard_map/ppermute | solution.py:22
  154.4 20.6 %collective-permute-start.36 = (bf16[128,1536]{1,0:T(8,128)(2,1)S(1)}, bf16[128,1536]{1,0:T(8,128)(2,1)S(1)}, u32[]{:S(2)}, u32[]{:S(2)}) collective-permute-start(bf16[128,1536]{1,0:T(8,128)(2,1)S(1)} %pad_maximum_fusion.4), channel_id=1, source_target_pairs={{0,48},{16,0},{32,16},{48,32},{1,49},{17,1},{33,17},{49,33},{2,50}... | collective-permute-start | bytes 1179656 | tf_op jit(solution)/shard_map/ppermute | solution.py:22
  155.9 12.6 %collective-permute-start.42 = (bf16[512,256]{1,0:T(8,128)(2,1)S(1)}, bf16[512,256]{1,0:T(8,128)(2,1)S(1)}, u32[]{:S(2)}, u32[]{:S(2)}) collective-permute-start(bf16[512,256]{1,0:T(8,128)(2,1)S(1)} %collective-permute-done.32), channel_id=1, source_target_pairs={{0,1},{1,0},{2,3},{3,2},{4,5},{5,4},{6,7},{7,6},{8,9},{9,8},{10,11... | collective-permute-start | bytes 786440 | tf_op jit(solution)/shard_map/ppermute | solution.py:22
  159.6 7.4 %collective-permute-start.41 = (bf16[512,256]{1,0:T(8,128)(2,1)S(1)}, bf16[512,256]{1,0:T(8,128)(2,1)S(1)}, u32[]{:S(2)}, u32[]{:S(2)}) collective-permute-start(bf16[512,256]{1,0:T(8,128)(2,1)S(1)} %collective-permute-done.40), channel_id=1, source_target_pairs={{0,6},{2,0},{4,2},{6,4},{1,7},{3,1},{5,3},{7,5},{8,14},{10,8},{12,... | collective-permute-start | bytes 786440 | tf_op jit(solution)/shard_map/ppermute | solution.py:22
  160.2 8.3 %collective-permute-start.43 = (bf16[512,256]{1,0:T(8,128)(2,1)S(1)}, bf16[512,256]{1,0:T(8,128)(2,1)S(1)}, u32[]{:S(2)}, u32[]{:S(2)}) collective-permute-start(bf16[512,256]{1,0:T(8,128)(2,1)S(1)} %collective-permute-done.40), channel_id=1, source_target_pairs={{0,2},{2,4},{4,6},{6,0},{1,3},{3,5},{5,7},{7,1},{8,10},{10,12},{12... | collective-permute-start | bytes 786440 | tf_op jit(solution)/shard_map/ppermute | solution.py:22
  167.0 19.6 %collective-permute-start.38 = (bf16[64,1536]{1,0:T(8,128)(2,1)S(1)}, bf16[64,1536]{1,0:T(8,128)(2,1)S(1)}, u32[]{:S(2)}, u32[]{:S(2)}) collective-permute-start(bf16[64,1536]{1,0:T(8,128)(2,1)S(1)} %fusion.56), channel_id=1, source_target_pairs={{0,32},{16,48},{32,0},{48,16},{1,33},{17,49},{33,1},{49,17},{2,34}... | collective-permute-start | bytes 589832 | tf_op jit(solution)/shard_map/ppermute | solution.py:22
  170.4 6.8 %collective-permute-start.46 = (bf16[64,1536]{1,0:T(8,128)(2,1)S(1)}, bf16[64,1536]{1,0:T(8,128)(2,1)S(1)}, u32[]{:S(2)}, u32[]{:S(2)}) collective-permute-start(bf16[64,1536]{1,0:T(8,128)(2,1)S(1)} %get-tuple-element.28), channel_id=1, source_target_pairs={{0,64},{64,0},{1,65},{65,1},{2,66},{66,2},{3,67},{67,3},{4,68},{68... | collective-permute-start | bytes 589832 | tf_op jit(solution)/shard_map/ppermute | solution.py:22
  171.5 12.9 %collective-permute-start.44 = (bf16[128,1536]{1,0:T(8,128)(2,1)S(1)}, bf16[128,1536]{1,0:T(8,128)(2,1)S(1)}, u32[]{:S(2)}, u32[]{:S(2)}) collective-permute-start(bf16[128,1536]{1,0:T(8,128)(2,1)S(1)} %pad_maximum_fusion.5), channel_id=1, source_target_pairs={{0,16},{16,32},{32,48},{48,0},{1,17},{17,33},{33,49},{49,1},{2,18}... | collective-permute-start | bytes 1179656 | tf_op jit(solution)/shard_map/ppermute | solution.py:22
  172.7 12.6 %collective-permute-start.45 = (bf16[128,1536]{1,0:T(8,128)(2,1)S(1)}, bf16[128,1536]{1,0:T(8,128)(2,1)S(1)}, u32[]{:S(2)}, u32[]{:S(2)}) collective-permute-start(bf16[128,1536]{1,0:T(8,128)(2,1)S(1)} %pad_maximum_fusion.6), channel_id=1, source_target_pairs={{0,48},{16,0},{32,16},{48,32},{1,49},{17,1},{33,17},{49,33},{2,50}... | collective-permute-start | bytes 1179656 | tf_op jit(solution)/shard_map/ppermute | solution.py:22
  175.2 11.4 %collective-permute-start.39 = (bf16[64,1536]{1,0:T(8,128)(2,1)S(1)}, bf16[64,1536]{1,0:T(8,128)(2,1)S(1)}, u32[]{:S(2)}, u32[]{:S(2)}) collective-permute-start(bf16[64,1536]{1,0:T(8,128)(2,1)S(1)} %fusion.55), channel_id=1, source_target_pairs={{0,64},{64,0},{1,65},{65,1},{2,66},{66,2},{3,67},{67,3},{4,68},{68... | collective-permute-start | bytes 589832 | tf_op jit(solution)/shard_map/ppermute | solution.py:22
  177.2 9.5 %collective-permute-start.47 = (bf16[64,1536]{1,0:T(8,128)(2,1)S(1)}, bf16[64,1536]{1,0:T(8,128)(2,1)S(1)}, u32[]{:S(2)}, u32[]{:S(2)}) collective-permute-start(bf16[64,1536]{1,0:T(8,128)(2,1)S(1)} %fusion.52), channel_id=1, source_target_pairs={{0,32},{16,48},{32,0},{48,16},{1,33},{17,49},{33,1},{49,17},{2,34}... | collective-permute-start | bytes 589832 | tf_op jit(solution)/shard_map/ppermute | solution.py:22
  185.4 5.8 %collective-permute-start.48 = (bf16[64,1536]{1,0:T(8,128)(2,1)S(1)}, bf16[64,1536]{1,0:T(8,128)(2,1)S(1)}, u32[]{:S(2)}, u32[]{:S(2)}) collective-permute-start(bf16[64,1536]{1,0:T(8,128)(2,1)S(1)} %fusion.51), channel_id=1, source_target_pairs={{0,64},{64,0},{1,65},{65,1},{2,66},{66,2},{3,67},{67,3},{4,68},{68... | collective-permute-start | bytes 589832 | tf_op jit(solution)/shard_map/ppermute | solution.py:22
  (10 other events, 62.7 us)

commit v2 on v1

--- a/solution.py
+++ b/solution.py
@@ -15,7 +15,7 @@
 BF16 = jnp.bfloat16
 CHUNKS = (((0, 0), (1, 0), (0, 1), (0, 3)), ((0, 2), (1, 1), (1, 3), (1, 2)))
 BLOCKS = tuple(b for chunk in CHUNKS for b in chunk)
-PIECES = ((0, (0, 1)), (1, (0,)), (1, (1,)))
+PIECES = ((0, (0,)), (0, (1,)), (1, (0,)), (1, (1,)))
 
 
 def move(x, axis, n, step):
@@ -195,12 +195,12 @@
     rows[1, 2] = swap(rows[0, 2], "zl")
 
     qs, ks, vs = [], [], []
-    for j, chunk in enumerate(CHUNKS):
+    for chunk in CHUNKS:
         own = [rows[b] for b in chunk]
         other = [swap(rows[dz, dy], "c") for dz, dy in chunk]
         parts = [product(jnp.concatenate(blocks), w_qkv) for blocks in (own, other)]
         first, second = reduce_over_x(*parts)
-        for summed in (jnp.concatenate([first, second]),) if j == 0 else (first, second):
+        for summed in (first, second):
             q, k, v = reduce_over_zh(summed, zh)
             qs.append(q)
             ks.append(k)

time: 195 us -> 207 us (1.062)
  starting transfers between devices: 61.9 us -> 74.7 us
  matrix products: 15.6 us -> 24.2 us
  waiting for transfers between devices: 80.1 us -> 72.3 us
  other arithmetic: 19.8 us -> 16.3 us
    ppermute x49 -> x50, starting transfers between devices: 61.9 us -> 74.7 us  [move(): return lax.ppermute(x, axis, [(i, (i + step) % n) for i in range(n)])]
    dot_general x6, matrix products: 15.6 us -> 24.2 us  [product(): full = jnp.dot(lhs, rhs, preferred_element_type=F32)]
    ppermute x49 -> x50, waiting for transfers between devices: 80.1 us -> 72.3 us  [move(): return lax.ppermute(x, axis, [(i, (i + step) % n) for i in range(n)])]
    concatenate x3 -> x4, other arithmetic: 4.55 us -> 2.69 us  [reduce_over_zh(): sent = jnp.concatenate([k, v, other_q]).astype(BF16)]
  transfers between devices with their start and end apart: 49 -> 50, of which waited for: 22 -> 21; matrix products, arithmetic and copies ran while one was open for 21% -> 22% of each run, Pallas kernels for 3% -> 3%
where the time goes in v2:
time: 207 us; the launch traced here: 204 us
  starting transfers between devices  74.7 us (36%)
  waiting for transfers between devices  72.3 us (35%)
  matrix products  24.2 us (12%)
  other arithmetic  16.3 us (8%)
  local copies, waits for them, and re-layouts  9.58 us (5%)
  Pallas kernels  5.98 us (3%)
    ppermute x50, starting transfers between devices, move(): return lax.ppermute(x, axis, [(i, (i + step) % n) for i in range(n)])  74.7 us
    ppermute x50, waiting for transfers between devices, move(): return lax.ppermute(x, axis, [(i, (i + step) % n) for i in range(n)])  72.3 us
    dot_general x6, matrix products, product(): full = jnp.dot(lhs, rhs, preferred_element_type=F32)  24.2 us
    pallas_call x1, Pallas kernels, attention(): pl.pallas_call(attend_body, grid_spec=pltpu.PrefetchScalarGridSpec(num_sc...  4.51 us
    unnamed x22, local copies, waits for them, and re-layouts  4.24 us
  transfers between devices with their start and end apart: 50, of which 21 were waited for; matrix products, arithmetic and copies ran while one was open for 22% of the time, Pallas kernels for 3%

profile of v2, /device:TPU:4, one launch (start us, length us, event | category | flops | bytes accessed | tf_op | source)
XLA Modules:
  0.0 203.7 jit_solution(12936918012717660106)
XLA Ops:
  0.0 1.9 collective-permute-start
  1.9 3.2 %collective-permute-start.15 = (bf16[128,1536]{1,0:T(8,128)(2,1)}, bf16[128,1536]{1,0:T(8,128)(2,1)}, u32[]{:S(2)}, u32[]{:S(2)}) collective-permute-start(bf16[128,1536]{1,0:T(8,128)(2,1)} %param.3), channel_id=1, source_target_pairs={{0,32},{16,48},{32,0},{48,16},{1,33},{17,49},{33,1},{49,17},{2,34}... | collective-permute-start | bytes 1179656 | tf_op jit(solution)/shard_map/ppermute | solution.py:22
  5.8 2.6 %collective-permute-start.1 = (bf16[128,1536]{1,0:T(8,128)(2,1)}, bf16[128,1536]{1,0:T(8,128)(2,1)S(1)}, u32[]{:S(2)}, u32[]{:S(2)}) collective-permute-start(bf16[128,1536]{1,0:T(8,128)(2,1)} %param.3), channel_id=1, source_target_pairs={{0,48},{16,0},{32,16},{48,32},{1,49},{17,1},{33,17},{49,33},{2,50}... | collective-permute-start | bytes 1179656 | tf_op jit(solution)/shard_map/ppermute | solution.py:22
  8.4 2.3 %copy-done = bf16[1536,3,512]{2,0,1:T(8,128)(2,1)S(1)} copy-done((bf16[1536,3,512]{2,0,1:T(8,128)(2,1)S(1)}, bf16[1536,3,512]{2,0,1:T(8,128)(2,1)}, u32[]{:S(2)}) %copy-start) | copy-done | bytes 4718616
  12.4 1.9 collective-permute-start.16
  14.3 1.5 collective-permute-done.15
  15.8 1.6 collective-permute-start.17
  17.3 6.0 %collective-permute-done.2 = bf16[128,1536]{1,0:T(8,128)(2,1)} collective-permute-done((bf16[128,1536]{1,0:T(8,128)(2,1)}, bf16[128,1536]{1,0:T(8,128)(2,1)}, u32[]{:S(2)}, u32[]{:S(2)}) %collective-permute-start.2) | collective-permute-done | bytes 393248 | tf_op jit(solution)/shard_map/ppermute | solution.py:22
  24.4 3.6 %fusion.88 = (bf16[512,1536]{1,0:T(8,128)(2,1)S(1)}, f32[512,1536]{1,0:T(8,128)S(1)}) fusion(bf16[1536,1536]{1,0:T(8,128)(2,1)S(1)} %order.1, bf16[128,1536]{1,0:T(8,128)(2,1)} %collective-permute-done.2, bf16[128,1536]{1,0:T(8,128)(2,1)S(1)} %collective-permute-done.1, bf16[128,1536]{1,0:T(8,128)(2,1)S(1)} %collective-permute-done, ...), kind=kOutput, calls=%fused_computation.158 | convolution fusion | flops 2422996992 | bytes 11010048 | tf_op jit(solution)/shard_map/dot_general | solution.py:73
  29.4 2.2 %collective-permute-done.16 = bf16[128,1536]{1,0:T(8,128)(2,1)} collective-permute-done((bf16[128,1536]{1,0:T(8,128)(2,1)S(1)}, bf16[128,1536]{1,0:T(8,128)(2,1)}, u32[]{:S(2)}, u32[]{:S(2)}) %collective-permute-start.16) | collective-permute-done | bytes 393248 | tf_op jit(solution)/shard_map/ppermute | solution.py:22
  32.1 2.0 %collective-permute-done.18 = bf16[128,1536]{1,0:T(8,128)(2,1)} collective-permute-done((bf16[128,1536]{1,0:T(8,128)(2,1)}, bf16[128,1536]{1,0:T(8,128)(2,1)}, u32[]{:S(2)}, u32[]{:S(2)}) %collective-permute-start.18) | collective-permute-done | bytes 393248 | tf_op jit(solution)/shard_map/ppermute | solution.py:22
  34.1 5.7 %fusion.90 = (bf16[512,1536]{1,0:T(8,128)(2,1)S(1)}, f32[512,1536]{1,0:T(8,128)}) fusion(bf16[1536,1536]{1,0:T(8,128)(2,1)S(1)} %order.1, bf16[128,1536]{1,0:T(8,128)(2,1)} %collective-permute-done.18, bf16[128,1536]{1,0:T(8,128)(2,1)} %collective-permute-done.17, bf16[128,1536]{1,0:T(8,128)(2,1)} %collective-permute-done.16, ...), kind=kOutput, calls=%fused_computation.160 | convolution fusion | flops 2422996992 | bytes 11010048 | tf_op jit(solution)/shard_map/dot_general | solution.py:73
  41.6 1.5 collective-permute-start.19
  43.1 2.4 %collective-permute-start.4 = (bf16[512,384]{1,0:T(8,128)(2,1)S(1)}, bf16[512,384]{1,0:T(8,128)(2,1)S(1)}, u32[]{:S(2)}, u32[]{:S(2)}) collective-permute-start(bf16[512,384]{1,0:T(8,128)(2,1)S(1)} %fusion.46), channel_id=1, source_target_pairs={{0,2},{2,4},{4,6},{6,0},{1,3},{3,5},{5,7},{7,1},{8,10},{10,12},{12... | collective-permute-start | bytes 1179656 | tf_op jit(solution)/shard_map/ppermute | solution.py:22
  45.5 4.3 %fusion.89 = (bf16[512,1536]{1,0:T(8,128)(2,1)S(1)}, f32[512,1536]{1,0:T(8,128)}) fusion(bf16[1536,1536]{1,0:T(8,128)(2,1)S(1)} %order.1, bf16[128,1536]{1,0:T(8,128)(2,1)S(1)} %collective-permute-done.10, bf16[128,1536]{1,0:T(8,128)(2,1)S(1)} %collective-permute-done.9, bf16[128,1536]{1,0:T(8,128)(2,1)S(1)} %collective-permute-done.8, ...), kind=kOutput, calls=%fused_computation.159 | convolution fusion | flops 2422996992 | bytes 11010048 | tf_op jit(solution)/shard_map/dot_general | solution.py:73
  50.7 1.4 collective-permute-done.5
  52.1 9.2 %collective-permute-done.4 = bf16[512,384]{1,0:T(8,128)(2,1)S(1)} collective-permute-done((bf16[512,384]{1,0:T(8,128)(2,1)S(1)}, bf16[512,384]{1,0:T(8,128)(2,1)S(1)}, u32[]{:S(2)}, u32[]{:S(2)}) %collective-permute-start.4) | collective-permute-done | bytes 393248 | tf_op jit(solution)/shard_map/ppermute | solution.py:22
  63.5 1.6 collective-permute-start.21
  65.1 3.0 %collective-permute-start.12 = (bf16[512,384]{1,0:T(8,128)(2,1)}, bf16[512,384]{1,0:T(8,128)(2,1)S(1)}, u32[]{:S(2)}, u32[]{:S(2)}) collective-permute-start(bf16[512,384]{1,0:T(8,128)(2,1)} %get-tuple-element.40), channel_id=1, source_target_pairs={{0,6},{2,0},{4,2},{6,4},{1,7},{3,1},{5,3},{7,5},{8,14},{10,8},{12,... | collective-permute-start | bytes 1179656 | tf_op jit(solution)/shard_map/ppermute | solution.py:22
  68.1 3.7 %collective-permute-start.6 = (bf16[1280,128]{1,0:T(8,128)(2,1)S(1)}, bf16[1280,128]{1,0:T(8,128)(2,1)S(1)}, u32[]{:S(2)}, u32[]{:S(2)}) collective-permute-start(bf16[1280,128]{1,0:T(8,128)(2,1)S(1)} %pad_maximum_fusion.5), channel_id=1, source_target_pairs={{0,1},{1,0},{2,3},{3,2},{4,5},{5,4},{6,7},{7,6},{8,9},{9,8},{10,11... | collective-permute-start | bytes 983048 | tf_op jit(solution)/shard_map/ppermute | solution.py:22
  71.8 7.1 %fusion.91 = (bf16[512,1536]{1,0:T(8,128)(2,1)S(1)}, f32[512,1536]{1,0:T(8,128)}) fusion(bf16[1536,1536]{1,0:T(8,128)(2,1)} %copy-done.1, bf16[128,1536]{1,0:T(8,128)(2,1)} %collective-permute-done.26, bf16[128,1536]{1,0:T(8,128)(2,1)} %collective-permute-done.25, bf16[128,1536]{1,0:T(8,128)(2,1)} %collective-permute-done.24, ...), kind=kOutput, calls=%fused_computation.161 | convolution fusion | flops 2422996992 | bytes 11010048 | tf_op jit(solution)/shard_map/dot_general | solution.py:73
  79.8 3.4 %collective-permute-done.12 = bf16[512,384]{1,0:T(8,128)(2,1)S(1)} collective-permute-done((bf16[512,384]{1,0:T(8,128)(2,1)}, bf16[512,384]{1,0:T(8,128)(2,1)S(1)}, u32[]{:S(2)}, u32[]{:S(2)}) %collective-permute-start.12) | collective-permute-done | bytes 393248 | tf_op jit(solution)/shard_map/ppermute | solution.py:22
  83.2 2.1 %collective-permute-start.28 = (bf16[512,384]{1,0:T(8,128)(2,1)}, bf16[512,384]{1,0:T(8,128)(2,1)}, u32[]{:S(2)}, u32[]{:S(2)}) collective-permute-start(bf16[512,384]{1,0:T(8,128)(2,1)} %get-tuple-element.36), channel_id=1, source_target_pairs={{0,6},{2,0},{4,2},{6,4},{1,7},{3,1},{5,3},{7,5},{8,14},{10,8},{12,... | collective-permute-start | bytes 1179656 | tf_op jit(solution)/shard_map/ppermute | solution.py:22
  87.0 3.3 %collective-permute-start.27 = (bf16[512,384]{1,0:T(8,128)(2,1)}, bf16[512,384]{1,0:T(8,128)(2,1)}, u32[]{:S(2)}, u32[]{:S(2)}) collective-permute-start(bf16[512,384]{1,0:T(8,128)(2,1)} %get-tuple-element.35), channel_id=1, source_target_pairs={{0,2},{2,4},{4,6},{6,0},{1,3},{3,5},{5,7},{7,1},{8,10},{10,12},{12... | collective-permute-start | bytes 1179656 | tf_op jit(solution)/shard_map/ppermute | solution.py:22
  90.3 7.6 %collective-permute-done.20 = bf16[512,384]{1,0:T(8,128)(2,1)S(1)} collective-permute-done((bf16[512,384]{1,0:T(8,128)(2,1)S(1)}, bf16[512,384]{1,0:T(8,128)(2,1)S(1)}, u32[]{:S(2)}, u32[]{:S(2)}) %collective-permute-start.20) | collective-permute-done | bytes 393248 | tf_op jit(solution)/shard_map/ppermute | solution.py:22
  97.9 2.0 collective-permute-start.13
  101.2 4.4 %collective-permute-done.13 = bf16[512,384]{1,0:T(8,128)(2,1)S(1)} collective-permute-done((bf16[512,384]{1,0:T(8,128)(2,1)S(1)}, bf16[512,384]{1,0:T(8,128)(2,1)S(1)}, u32[]{:S(2)}, u32[]{:S(2)}) %collective-permute-start.13) | collective-permute-done | bytes 393248 | tf_op jit(solution)/shard_map/ppermute | solution.py:22
  108.2 3.6 %collective-permute-start.22 = (bf16[1280,128]{1,0:T(8,128)(2,1)}, bf16[1280,128]{1,0:T(8,128)(2,1)}, u32[]{:S(2)}, u32[]{:S(2)}) collective-permute-start(bf16[1280,128]{1,0:T(8,128)(2,1)} %pad_maximum_fusion.7), channel_id=1, source_target_pairs={{0,1},{1,0},{2,3},{3,2},{4,5},{5,4},{6,7},{7,6},{8,9},{9,8},{10,11... | collective-permute-start | bytes 983048 | tf_op jit(solution)/shard_map/ppermute | solution.py:22
  114.4 2.3 %collective-permute-start.29 = (bf16[512,384]{1,0:T(8,128)(2,1)S(1)}, bf16[512,384]{1,0:T(8,128)(2,1)S(1)}, u32[]{:S(2)}, u32[]{:S(2)}) collective-permute-start(bf16[512,384]{1,0:T(8,128)(2,1)S(1)} %fusion.40), channel_id=1, source_target_pairs={{0,6},{2,0},{4,2},{6,4},{1,7},{3,1},{5,3},{7,5},{8,14},{10,8},{12,... | collective-permute-start | bytes 1179656 | tf_op jit(solution)/shard_map/ppermute | solution.py:22
  116.7 3.0 %collective-permute-done.22 = bf16[1280,128]{1,0:T(8,128)(2,1)} collective-permute-done((bf16[1280,128]{1,0:T(8,128)(2,1)}, bf16[1280,128]{1,0:T(8,128)(2,1)}, u32[]{:S(2)}, u32[]{:S(2)}) %collective-permute-start.22) | collective-permute-done | bytes 327712 | tf_op jit(solution)/shard_map/ppermute | solution.py:22
  120.8 2.3 %collective-permute-done.14 = bf16[1280,128]{1,0:T(8,128)(2,1)S(1)} collective-permute-done((bf16[1280,128]{1,0:T(8,128)(2,1)S(1)}, bf16[1280,128]{1,0:T(8,128)(2,1)S(1)}, u32[]{:S(2)}, u32[]{:S(2)}) %collective-permute-start.14) | collective-permute-done | bytes 327712 | tf_op jit(solution)/shard_map/ppermute | solution.py:22
  128.8 3.0 %collective-permute-start.30 = (bf16[1280,128]{1,0:T(8,128)(2,1)S(1)}, bf16[1280,128]{1,0:T(8,128)(2,1)S(1)}, u32[]{:S(2)}, u32[]{:S(2)}) collective-permute-start(bf16[1280,128]{1,0:T(8,128)(2,1)S(1)} %pad_maximum_fusion.8), channel_id=1, source_target_pairs={{0,1},{1,0},{2,3},{3,2},{4,5},{5,4},{6,7},{7,6},{8,9},{9,8},{10,11... | collective-permute-start | bytes 983048 | tf_op jit(solution)/shard_map/ppermute | solution.py:22
  133.7 3.8 %collective-permute-done.30 = bf16[1280,128]{1,0:T(8,128)(2,1)S(1)} collective-permute-done((bf16[1280,128]{1,0:T(8,128)(2,1)S(1)}, bf16[1280,128]{1,0:T(8,128)(2,1)S(1)}, u32[]{:S(2)}, u32[]{:S(2)}) %collective-permute-start.30) | collective-permute-done | bytes 327712 | tf_op jit(solution)/shard_map/ppermute | solution.py:22
  137.6 4.5 %attend.1 = (bf16[512,128]{1,0:T(8,128)(2,1)S(1)}, bf16[512,128]{1,0:T(8,128)(2,1)S(1)}) custom-call(s32[4]{0:T(128)S(1)} %pad_add_fusion.at_ref, bf16[256,128]{1,0:T(8,128)(2,1)S(1)} %fusion.68.refs_0_, bf16[256,128]{1,0:T(8,128)(2,1)S(1)} %fusion.67.refs_1_, bf16[256,128]{1,0:T(8,128)(2,1)S(1)} %fusion.66.refs_2_, bf16[256,128]{1,0:T(8,128)(2,1)S(1)} %fusion.65.refs_3_, ...), custom_call_target="tpu_custom_call" | custom-call | tf_op jit(solution)/shard_map/attend/pallas_call | solution.py:111
  143.6 4.1 %collective-permute-start.33 = (bf16[512,256]{1,0:T(8,128)(2,1)S(1)}, bf16[512,256]{1,0:T(8,128)(2,1)S(1)}, u32[]{:S(2)}, u32[]{:S(2)}) collective-permute-start(bf16[512,256]{1,0:T(8,128)(2,1)S(1)} %get-tuple-element.62), channel_id=1, source_target_pairs={{0,4},{2,6},{4,0},{6,2},{1,5},{3,7},{5,1},{7,3},{8,12},{10,14},{12... | collective-permute-start | bytes 786440 | tf_op jit(solution)/shard_map/ppermute | solution.py:22
  149.8 1.6 pad_maximum_fusion
  151.4 3.2 %collective-permute-start.41 = (bf16[512,256]{1,0:T(8,128)(2,1)S(1)}, bf16[512,256]{1,0:T(8,128)(2,1)S(1)}, u32[]{:S(2)}, u32[]{:S(2)}) collective-permute-start(bf16[512,256]{1,0:T(8,128)(2,1)S(1)} %get-tuple-element.62), channel_id=1, source_target_pairs={{0,1},{1,0},{2,3},{3,2},{4,5},{5,4},{6,7},{7,6},{8,9},{9,8},{10,11... | collective-permute-start | bytes 786440 | tf_op jit(solution)/shard_map/ppermute | solution.py:22
  154.6 5.2 %collective-permute-done.32 = bf16[512,256]{1,0:T(8,128)(2,1)S(1)} collective-permute-done((bf16[512,256]{1,0:T(8,128)(2,1)S(1)}, bf16[512,256]{1,0:T(8,128)(2,1)S(1)}, u32[]{:S(2)}, u32[]{:S(2)}) %collective-permute-start.32) | collective-permute-done | bytes 262176 | tf_op jit(solution)/shard_map/ppermute | solution.py:22
  160.0 1.8 fusion.92
  162.6 2.9 %collective-permute-start.37 = (bf16[128,1536]{1,0:T(8,128)(2,1)S(1)}, bf16[128,1536]{1,0:T(8,128)(2,1)S(1)}, u32[]{:S(2)}, u32[]{:S(2)}) collective-permute-start(bf16[128,1536]{1,0:T(8,128)(2,1)S(1)} %pad_maximum_fusion.2), channel_id=1, source_target_pairs={{0,48},{16,0},{32,16},{48,32},{1,49},{17,1},{33,17},{49,33},{2,50}... | collective-permute-start | bytes 1179656 | tf_op jit(solution)/shard_map/ppermute | solution.py:22
  165.4 3.3 %collective-permute-start.43 = (bf16[512,256]{1,0:T(8,128)(2,1)S(1)}, bf16[512,256]{1,0:T(8,128)(2,1)S(1)}, u32[]{:S(2)}, u32[]{:S(2)}) collective-permute-start(bf16[512,256]{1,0:T(8,128)(2,1)S(1)} %collective-permute-done.33), channel_id=1, source_target_pairs={{0,1},{1,0},{2,3},{3,2},{4,5},{5,4},{6,7},{7,6},{8,9},{9,8},{10,11... | collective-permute-start | bytes 786440 | tf_op jit(solution)/shard_map/ppermute | solution.py:22
  170.0 1.4 collective-permute-start.44
  171.5 5.2 %collective-permute-done.42 = bf16[512,256]{1,0:T(8,128)(2,1)S(1)} collective-permute-done((bf16[512,256]{1,0:T(8,128)(2,1)S(1)}, bf16[512,256]{1,0:T(8,128)(2,1)S(1)}, u32[]{:S(2)}, u32[]{:S(2)}) %collective-permute-start.42) | collective-permute-done | bytes 262176 | tf_op jit(solution)/shard_map/ppermute | solution.py:22
  177.6 1.8 fusion.93
  181.1 2.9 %collective-permute-start.46 = (bf16[128,1536]{1,0:T(8,128)(2,1)S(1)}, bf16[128,1536]{1,0:T(8,128)(2,1)S(1)}, u32[]{:S(2)}, u32[]{:S(2)}) collective-permute-start(bf16[128,1536]{1,0:T(8,128)(2,1)S(1)} %pad_maximum_fusion.4), channel_id=1, source_target_pairs={{0,48},{16,0},{32,16},{48,32},{1,49},{17,1},{33,17},{49,33},{2,50}... | collective-permute-start | bytes 1179656 | tf_op jit(solution)/shard_map/ppermute | solution.py:22
  186.4 3.6 %collective-permute-start.48 = (bf16[64,1536]{1,0:T(8,128)(2,1)S(1)}, bf16[64,1536]{1,0:T(8,128)(2,1)S(1)}, u32[]{:S(2)}, u32[]{:S(2)}) collective-permute-start(bf16[64,1536]{1,0:T(8,128)(2,1)S(1)} %fusion.50), channel_id=1, source_target_pairs={{0,32},{16,48},{32,0},{48,16},{1,33},{17,49},{33,1},{49,17},{2,34}... | collective-permute-start | bytes 589832 | tf_op jit(solution)/shard_map/ppermute | solution.py:22
  190.0 6.7 %collective-permute-done.45 = bf16[128,1536]{1,0:T(8,128)(2,1)S(1)} collective-permute-done((bf16[128,1536]{1,0:T(8,128)(2,1)S(1)}, bf16[128,1536]{1,0:T(8,128)(2,1)S(1)}, u32[]{:S(2)}, u32[]{:S(2)}) %collective-permute-start.45) | collective-permute-done | bytes 393248 | tf_op jit(solution)/shard_map/ppermute | solution.py:22
  198.2 4.5 %collective-permute-done.49 = bf16[64,1536]{1,0:T(8,128)(2,1)S(1)} collective-permute-done((bf16[64,1536]{1,0:T(8,128)(2,1)S(1)}, bf16[64,1536]{1,0:T(8,128)(2,1)S(1)}, u32[]{:S(2)}, u32[]{:S(2)}) %collective-permute-start.49) | collective-permute-done | bytes 196640 | tf_op jit(solution)/shard_map/ppermute | solution.py:22
  (148 shorter events, 40.8 us)
Async XLA Ops:
  0.0 12.4 %collective-permute-start = (bf16[128,1536]{1,0:T(8,128)(2,1)}, bf16[128,1536]{1,0:T(8,128)(2,1)S(1)}, u32[]{:S(2)}, u32[]{:S(2)}) collective-permute-start(bf16[128,1536]{1,0:T(8,128)(2,1)} %param.3), channel_id=1, source_target_pairs={{0,64},{64,0},{1,65},{65,1},{2,66},{66,2},{3,67},{67,3},{4,68},{68... | collective-permute-start | bytes 1179656 | tf_op jit(solution)/shard_map/ppermute | solution.py:22
  1.9 13.8 %collective-permute-start.15 = (bf16[128,1536]{1,0:T(8,128)(2,1)}, bf16[128,1536]{1,0:T(8,128)(2,1)}, u32[]{:S(2)}, u32[]{:S(2)}) collective-permute-start(bf16[128,1536]{1,0:T(8,128)(2,1)} %param.3), channel_id=1, source_target_pairs={{0,32},{16,48},{32,0},{48,16},{1,33},{17,49},{33,1},{49,17},{2,34}... | collective-permute-start | bytes 1179656 | tf_op jit(solution)/shard_map/ppermute | solution.py:22
  5.1 18.2 %collective-permute-start.2 = (bf16[128,1536]{1,0:T(8,128)(2,1)}, bf16[128,1536]{1,0:T(8,128)(2,1)}, u32[]{:S(2)}, u32[]{:S(2)}) collective-permute-start(bf16[128,1536]{1,0:T(8,128)(2,1)} %param.3), channel_id=1, source_target_pairs={{0,16},{16,32},{32,48},{48,0},{1,17},{17,33},{33,49},{49,1},{2,18}... | collective-permute-start | bytes 1179656 | tf_op jit(solution)/shard_map/ppermute | solution.py:22
  5.8 18.6 %collective-permute-start.1 = (bf16[128,1536]{1,0:T(8,128)(2,1)}, bf16[128,1536]{1,0:T(8,128)(2,1)S(1)}, u32[]{:S(2)}, u32[]{:S(2)}) collective-permute-start(bf16[128,1536]{1,0:T(8,128)(2,1)} %param.3), channel_id=1, source_target_pairs={{0,48},{16,0},{32,16},{48,32},{1,49},{17,1},{33,17},{49,33},{2,50}... | collective-permute-start | bytes 1179656 | tf_op jit(solution)/shard_map/ppermute | solution.py:22
  8.4 32.9 %collective-permute-start.7 = (bf16[128,1536]{1,0:T(8,128)(2,1)}, bf16[128,1536]{1,0:T(8,128)(2,1)S(1)}, u32[]{:S(2)}, u32[]{:S(2)}) collective-permute-start(bf16[128,1536]{1,0:T(8,128)(2,1)} %param.3), channel_id=1, source_target_pairs={{0,8},{8,0},{1,9},{9,1},{2,10},{10,2},{3,11},{11,3},{4,12},{12,4},... | collective-permute-start | bytes 1179656 | tf_op jit(solution)/shard_map/ppermute | solution.py:22
  12.4 19.2 %collective-permute-start.16 = (bf16[128,1536]{1,0:T(8,128)(2,1)S(1)}, bf16[128,1536]{1,0:T(8,128)(2,1)}, u32[]{:S(2)}, u32[]{:S(2)}) collective-permute-start(bf16[128,1536]{1,0:T(8,128)(2,1)S(1)} %collective-permute-done), channel_id=1, source_target_pairs={{0,48},{16,0},{32,16},{48,32},{1,49},{17,1},{33,17},{49,33},{2,50}... | collective-permute-start | bytes 1179656 | tf_op jit(solution)/shard_map/ppermute | solution.py:22
  15.8 15.8 %collective-permute-start.17 = (bf16[128,1536]{1,0:T(8,128)(2,1)S(1)}, bf16[128,1536]{1,0:T(8,128)(2,1)}, u32[]{:S(2)}, u32[]{:S(2)}) collective-permute-start(bf16[128,1536]{1,0:T(8,128)(2,1)S(1)} %collective-permute-done), channel_id=1, source_target_pairs={{0,16},{16,32},{32,48},{48,0},{1,17},{17,33},{33,49},{49,1},{2,18}... | collective-permute-start | bytes 1179656 | tf_op jit(solution)/shard_map/ppermute | solution.py:22
  23.4 10.8 %collective-permute-start.18 = (bf16[128,1536]{1,0:T(8,128)(2,1)}, bf16[128,1536]{1,0:T(8,128)(2,1)}, u32[]{:S(2)}, u32[]{:S(2)}) collective-permute-start(bf16[128,1536]{1,0:T(8,128)(2,1)} %collective-permute-done.15), channel_id=1, source_target_pairs={{0,64},{64,0},{1,65},{65,1},{2,66},{66,2},{3,67},{67,3},{4,68},{68... | collective-permute-start | bytes 1179656 | tf_op jit(solution)/shard_map/ppermute | solution.py:22
  28.1 12.5 %collective-permute-start.3 = (bf16[512,384]{1,0:T(8,128)(2,1)S(1)}, bf16[512,384]{1,0:T(8,128)(2,1)S(1)}, u32[]{:S(2)}, u32[]{:S(2)}) collective-permute-start(bf16[512,384]{1,0:T(8,128)(2,1)S(1)} %get-tuple-element.41), channel_id=1, source_target_pairs={{0,2},{2,4},{4,6},{6,0},{1,3},{3,5},{5,7},{7,1},{8,10},{10,12},{12... | collective-permute-start | bytes 1179656 | tf_op jit(solution)/shard_map/ppermute | solution.py:22
  31.6 10.0 %collective-permute-start.8 = (bf16[128,1536]{1,0:T(8,128)(2,1)S(1)}, bf16[128,1536]{1,0:T(8,128)(2,1)S(1)}, u32[]{:S(2)}, u32[]{:S(2)}) collective-permute-start(bf16[128,1536]{1,0:T(8,128)(2,1)S(1)} %collective-permute-done), channel_id=1, source_target_pairs={{0,8},{8,0},{1,9},{9,1},{2,10},{10,2},{3,11},{11,3},{4,12},{12,4},... | collective-permute-start | bytes 1179656 | tf_op jit(solution)/shard_map/ppermute | solution.py:22
  31.6 11.5 %collective-permute-start.10 = (bf16[128,1536]{1,0:T(8,128)(2,1)}, bf16[128,1536]{1,0:T(8,128)(2,1)S(1)}, u32[]{:S(2)}, u32[]{:S(2)}) collective-permute-start(bf16[128,1536]{1,0:T(8,128)(2,1)} %collective-permute-done.2), channel_id=1, source_target_pairs={{0,8},{8,0},{1,9},{9,1},{2,10},{10,2},{3,11},{11,3},{4,12},{12,4},... | collective-permute-start | bytes 1179656 | tf_op jit(solution)/shard_map/ppermute | solution.py:22
  34.1 11.4 %collective-permute-start.9 = (bf16[128,1536]{1,0:T(8,128)(2,1)S(1)}, bf16[128,1536]{1,0:T(8,128)(2,1)S(1)}, u32[]{:S(2)}, u32[]{:S(2)}) collective-permute-start(bf16[128,1536]{1,0:T(8,128)(2,1)S(1)} %collective-permute-done.1), channel_id=1, source_target_pairs={{0,8},{8,0},{1,9},{9,1},{2,10},{10,2},{3,11},{11,3},{4,12},{12,4},... | collective-permute-start | bytes 1179656 | tf_op jit(solution)/shard_map/ppermute | solution.py:22
  40.6 11.5 %collective-permute-start.5 = (bf16[512,384]{1,0:T(8,128)(2,1)S(1)}, bf16[512,384]{1,0:T(8,128)(2,1)S(1)}, u32[]{:S(2)}, u32[]{:S(2)}) collective-permute-start(bf16[512,384]{1,0:T(8,128)(2,1)S(1)} %get-tuple-element.42), channel_id=1, source_target_pairs={{0,6},{2,0},{4,2},{6,4},{1,7},{3,1},{5,3},{7,5},{8,14},{10,8},{12,... | collective-permute-start | bytes 1179656 | tf_op jit(solution)/shard_map/ppermute | solution.py:22
  41.3 22.2 %collective-permute-start.23 = (bf16[128,1536]{1,0:T(8,128)(2,1)}, bf16[128,1536]{1,0:T(8,128)(2,1)}, u32[]{:S(2)}, u32[]{:S(2)}) collective-permute-start(bf16[128,1536]{1,0:T(8,128)(2,1)} %collective-permute-done.15), channel_id=1, source_target_pairs={{0,8},{8,0},{1,9},{9,1},{2,10},{10,2},{3,11},{11,3},{4,12},{12,4},... | collective-permute-start | bytes 1179656 | tf_op jit(solution)/shard_map/ppermute | solution.py:22
  41.6 20.0 %collective-permute-start.19 = (bf16[512,384]{1,0:T(8,128)(2,1)S(1)}, bf16[512,384]{1,0:T(8,128)(2,1)}, u32[]{:S(2)}, u32[]{:S(2)}) collective-permute-start(bf16[512,384]{1,0:T(8,128)(2,1)S(1)} %get-tuple-element.37), channel_id=1, source_target_pairs={{0,2},{2,4},{4,6},{6,0},{1,3},{3,5},{5,7},{7,1},{8,10},{10,12},{12... | collective-permute-start | bytes 1179656 | tf_op jit(solution)/shard_map/ppermute | solution.py:22
  43.1 18.2 %collective-permute-start.4 = (bf16[512,384]{1,0:T(8,128)(2,1)S(1)}, bf16[512,384]{1,0:T(8,128)(2,1)S(1)}, u32[]{:S(2)}, u32[]{:S(2)}) collective-permute-start(bf16[512,384]{1,0:T(8,128)(2,1)S(1)} %fusion.46), channel_id=1, source_target_pairs={{0,2},{2,4},{4,6},{6,0},{1,3},{3,5},{5,7},{7,1},{8,10},{10,12},{12... | collective-permute-start | bytes 1179656 | tf_op jit(solution)/shard_map/ppermute | solution.py:22
  45.5 19.6 %collective-permute-start.24 = (bf16[128,1536]{1,0:T(8,128)(2,1)}, bf16[128,1536]{1,0:T(8,128)(2,1)}, u32[]{:S(2)}, u32[]{:S(2)}) collective-permute-start(bf16[128,1536]{1,0:T(8,128)(2,1)} %collective-permute-done.16), channel_id=1, source_target_pairs={{0,8},{8,0},{1,9},{9,1},{2,10},{10,2},{3,11},{11,3},{4,12},{12,4},... | collective-permute-start | bytes 1179656 | tf_op jit(solution)/shard_map/ppermute | solution.py:22
  52.1 15.9 %collective-permute-start.25 = (bf16[128,1536]{1,0:T(8,128)(2,1)}, bf16[128,1536]{1,0:T(8,128)(2,1)}, u32[]{:S(2)}, u32[]{:S(2)}) collective-permute-start(bf16[128,1536]{1,0:T(8,128)(2,1)} %collective-permute-done.17), channel_id=1, source_target_pairs={{0,8},{8,0},{1,9},{9,1},{2,10},{10,2},{3,11},{11,3},{4,12},{12,4},... | collective-permute-start | bytes 1179656 | tf_op jit(solution)/shard_map/ppermute | solution.py:22
  61.3 6.8 %collective-permute-start.26 = (bf16[128,1536]{1,0:T(8,128)(2,1)}, bf16[128,1536]{1,0:T(8,128)(2,1)}, u32[]{:S(2)}, u32[]{:S(2)}) collective-permute-start(bf16[128,1536]{1,0:T(8,128)(2,1)} %collective-permute-done.18), channel_id=1, source_target_pairs={{0,8},{8,0},{1,9},{9,1},{2,10},{10,2},{3,11},{11,3},{4,12},{12,4},... | collective-permute-start | bytes 1179656 | tf_op jit(solution)/shard_map/ppermute | solution.py:22
  61.6 88.2 %collective-permute-start.35 = (bf16[512,1536]{1,0:T(8,128)(2,1)S(1)}, bf16[512,1536]{1,0:T(8,128)(2,1)}, u32[]{:S(2)}, u32[]{:S(2)}) collective-permute-start(bf16[512,1536]{1,0:T(8,128)(2,1)S(1)} %turn.1), channel_id=1, source_target_pairs={{0,8},{8,0},{1,9},{9,1},{2,10},{10,2},{3,11},{11,3},{4,12},{12,4},... | collective-permute-start | bytes 4718600 | tf_op jit(solution)/shard_map/ppermute | solution.py:22
  63.5 23.5 %collective-permute-start.21 = (bf16[512,384]{1,0:T(8,128)(2,1)}, bf16[512,384]{1,0:T(8,128)(2,1)S(1)}, u32[]{:S(2)}, u32[]{:S(2)}) collective-permute-start(bf16[512,384]{1,0:T(8,128)(2,1)} %get-tuple-element.38), channel_id=1, source_target_pairs={{0,6},{2,0},{4,2},{6,4},{1,7},{3,1},{5,3},{7,5},{8,14},{10,8},{12,... | collective-permute-start | bytes 1179656 | tf_op jit(solution)/shard_map/ppermute | solution.py:22
  65.1 18.1 %collective-permute-start.12 = (bf16[512,384]{1,0:T(8,128)(2,1)}, bf16[512,384]{1,0:T(8,128)(2,1)S(1)}, u32[]{:S(2)}, u32[]{:S(2)}) collective-permute-start(bf16[512,384]{1,0:T(8,128)(2,1)} %get-tuple-element.40), channel_id=1, source_target_pairs={{0,6},{2,0},{4,2},{6,4},{1,7},{3,1},{5,3},{7,5},{8,14},{10,8},{12,... | collective-permute-start | bytes 1179656 | tf_op jit(solution)/shard_map/ppermute | solution.py:22
  68.1 33.2 %collective-permute-start.11 = (bf16[512,384]{1,0:T(8,128)(2,1)}, bf16[512,384]{1,0:T(8,128)(2,1)S(1)}, u32[]{:S(2)}, u32[]{:S(2)}) collective-permute-start(bf16[512,384]{1,0:T(8,128)(2,1)} %get-tuple-element.39), channel_id=1, source_target_pairs={{0,2},{2,4},{4,6},{6,0},{1,3},{3,5},{5,7},{7,1},{8,10},{10,12},{12... | collective-permute-start | bytes 1179656 | tf_op jit(solution)/shard_map/ppermute | solution.py:22
  68.1 17.4 %collective-permute-start.6 = (bf16[1280,128]{1,0:T(8,128)(2,1)S(1)}, bf16[1280,128]{1,0:T(8,128)(2,1)S(1)}, u32[]{:S(2)}, u32[]{:S(2)}) collective-permute-start(bf16[1280,128]{1,0:T(8,128)(2,1)S(1)} %pad_maximum_fusion.5), channel_id=1, source_target_pairs={{0,1},{1,0},{2,3},{3,2},{4,5},{5,4},{6,7},{7,6},{8,9},{9,8},{10,11... | collective-permute-start | bytes 983048 | tf_op jit(solution)/shard_map/ppermute | solution.py:22
  83.2 29.7 %collective-permute-start.28 = (bf16[512,384]{1,0:T(8,128)(2,1)}, bf16[512,384]{1,0:T(8,128)(2,1)}, u32[]{:S(2)}, u32[]{:S(2)}) collective-permute-start(bf16[512,384]{1,0:T(8,128)(2,1)} %get-tuple-element.36), channel_id=1, source_target_pairs={{0,6},{2,0},{4,2},{6,4},{1,7},{3,1},{5,3},{7,5},{8,14},{10,8},{12,... | collective-permute-start | bytes 1179656 | tf_op jit(solution)/shard_map/ppermute | solution.py:22
  85.5 12.4 %collective-permute-start.20 = (bf16[512,384]{1,0:T(8,128)(2,1)S(1)}, bf16[512,384]{1,0:T(8,128)(2,1)S(1)}, u32[]{:S(2)}, u32[]{:S(2)}) collective-permute-start(bf16[512,384]{1,0:T(8,128)(2,1)S(1)} %fusion.42), channel_id=1, source_target_pairs={{0,2},{2,4},{4,6},{6,0},{1,3},{3,5},{5,7},{7,1},{8,10},{10,12},{12... | collective-permute-start | bytes 1179656 | tf_op jit(solution)/shard_map/ppermute | solution.py:22
  87.0 36.3 %collective-permute-start.27 = (bf16[512,384]{1,0:T(8,128)(2,1)}, bf16[512,384]{1,0:T(8,128)(2,1)}, u32[]{:S(2)}, u32[]{:S(2)}) collective-permute-start(bf16[512,384]{1,0:T(8,128)(2,1)} %get-tuple-element.35), channel_id=1, source_target_pairs={{0,2},{2,4},{4,6},{6,0},{1,3},{3,5},{5,7},{7,1},{8,10},{10,12},{12... | collective-permute-start | bytes 1179656 | tf_op jit(solution)/shard_map/ppermute | solution.py:22
  97.9 7.8 %collective-permute-start.13 = (bf16[512,384]{1,0:T(8,128)(2,1)S(1)}, bf16[512,384]{1,0:T(8,128)(2,1)S(1)}, u32[]{:S(2)}, u32[]{:S(2)}) collective-permute-start(bf16[512,384]{1,0:T(8,128)(2,1)S(1)} %fusion.44), channel_id=1, source_target_pairs={{0,6},{2,0},{4,2},{6,4},{1,7},{3,1},{5,3},{7,5},{8,14},{10,8},{12,... | collective-permute-start | bytes 1179656 | tf_op jit(solution)/shard_map/ppermute | solution.py:22
  108.2 11.5 %collective-permute-start.22 = (bf16[1280,128]{1,0:T(8,128)(2,1)}, bf16[1280,128]{1,0:T(8,128)(2,1)}, u32[]{:S(2)}, u32[]{:S(2)}) collective-permute-start(bf16[1280,128]{1,0:T(8,128)(2,1)} %pad_maximum_fusion.7), channel_id=1, source_target_pairs={{0,1},{1,0},{2,3},{3,2},{4,5},{5,4},{6,7},{7,6},{8,9},{9,8},{10,11... | collective-permute-start | bytes 983048 | tf_op jit(solution)/shard_map/ppermute | solution.py:22
  112.8 10.3 %collective-permute-start.14 = (bf16[1280,128]{1,0:T(8,128)(2,1)S(1)}, bf16[1280,128]{1,0:T(8,128)(2,1)S(1)}, u32[]{:S(2)}, u32[]{:S(2)}) collective-permute-start(bf16[1280,128]{1,0:T(8,128)(2,1)S(1)} %pad_maximum_fusion.6), channel_id=1, source_target_pairs={{0,1},{1,0},{2,3},{3,2},{4,5},{5,4},{6,7},{7,6},{8,9},{9,8},{10,11... | collective-permute-start | bytes 983048 | tf_op jit(solution)/shard_map/ppermute | solution.py:22
  114.4 9.7 %collective-permute-start.29 = (bf16[512,384]{1,0:T(8,128)(2,1)S(1)}, bf16[512,384]{1,0:T(8,128)(2,1)S(1)}, u32[]{:S(2)}, u32[]{:S(2)}) collective-permute-start(bf16[512,384]{1,0:T(8,128)(2,1)S(1)} %fusion.40), channel_id=1, source_target_pairs={{0,6},{2,0},{4,2},{6,4},{1,7},{3,1},{5,3},{7,5},{8,14},{10,8},{12,... | collective-permute-start | bytes 1179656 | tf_op jit(solution)/shard_map/ppermute | solution.py:22
  128.8 8.7 %collective-permute-start.30 = (bf16[1280,128]{1,0:T(8,128)(2,1)S(1)}, bf16[1280,128]{1,0:T(8,128)(2,1)S(1)}, u32[]{:S(2)}, u32[]{:S(2)}) collective-permute-start(bf16[1280,128]{1,0:T(8,128)(2,1)S(1)} %pad_maximum_fusion.8), channel_id=1, source_target_pairs={{0,1},{1,0},{2,3},{3,2},{4,5},{5,4},{6,7},{7,6},{8,9},{9,8},{10,11... | collective-permute-start | bytes 983048 | tf_op jit(solution)/shard_map/ppermute | solution.py:22
  143.6 16.2 %collective-permute-start.33 = (bf16[512,256]{1,0:T(8,128)(2,1)S(1)}, bf16[512,256]{1,0:T(8,128)(2,1)S(1)}, u32[]{:S(2)}, u32[]{:S(2)}) collective-permute-start(bf16[512,256]{1,0:T(8,128)(2,1)S(1)} %get-tuple-element.62), channel_id=1, source_target_pairs={{0,4},{2,6},{4,0},{6,2},{1,5},{3,7},{5,1},{7,3},{8,12},{10,14},{12... | collective-permute-start | bytes 786440 | tf_op jit(solution)/shard_map/ppermute | solution.py:22
  147.7 12.0 %collective-permute-start.32 = (bf16[512,256]{1,0:T(8,128)(2,1)S(1)}, bf16[512,256]{1,0:T(8,128)(2,1)S(1)}, u32[]{:S(2)}, u32[]{:S(2)}) collective-permute-start(bf16[512,256]{1,0:T(8,128)(2,1)S(1)} %get-tuple-element.62), channel_id=1, source_target_pairs={{0,6},{2,0},{4,2},{6,4},{1,7},{3,1},{5,3},{7,5},{8,14},{10,8},{12,... | collective-permute-start | bytes 786440 | tf_op jit(solution)/shard_map/ppermute | solution.py:22
  148.5 11.4 %collective-permute-start.34 = (bf16[512,256]{1,0:T(8,128)(2,1)S(1)}, bf16[512,256]{1,0:T(8,128)(2,1)S(1)}, u32[]{:S(2)}, u32[]{:S(2)}) collective-permute-start(bf16[512,256]{1,0:T(8,128)(2,1)S(1)} %get-tuple-element.62), channel_id=1, source_target_pairs={{0,2},{2,4},{4,6},{6,0},{1,3},{3,5},{5,7},{7,1},{8,10},{10,12},{12... | collective-permute-start | bytes 786440 | tf_op jit(solution)/shard_map/ppermute | solution.py:22
  151.4 17.3 %collective-permute-start.41 = (bf16[512,256]{1,0:T(8,128)(2,1)S(1)}, bf16[512,256]{1,0:T(8,128)(2,1)S(1)}, u32[]{:S(2)}, u32[]{:S(2)}) collective-permute-start(bf16[512,256]{1,0:T(8,128)(2,1)S(1)} %get-tuple-element.62), channel_id=1, source_target_pairs={{0,1},{1,0},{2,3},{3,2},{4,5},{5,4},{6,7},{7,6},{8,9},{9,8},{10,11... | collective-permute-start | bytes 786440 | tf_op jit(solution)/shard_map/ppermute | solution.py:22
  161.9 8.1 %collective-permute-start.38 = (bf16[64,1536]{1,0:T(8,128)(2,1)S(1)}, bf16[64,1536]{1,0:T(8,128)(2,1)S(1)}, u32[]{:S(2)}, u32[]{:S(2)}) collective-permute-start(bf16[64,1536]{1,0:T(8,128)(2,1)S(1)} %get-tuple-element.25), channel_id=1, source_target_pairs={{0,64},{64,0},{1,65},{65,1},{2,66},{66,2},{3,67},{67,3},{4,68},{68... | collective-permute-start | bytes 589832 | tf_op jit(solution)/shard_map/ppermute | solution.py:22
  162.0 19.1 %collective-permute-start.36 = (bf16[128,1536]{1,0:T(8,128)(2,1)S(1)}, bf16[128,1536]{1,0:T(8,128)(2,1)S(1)}, u32[]{:S(2)}, u32[]{:S(2)}) collective-permute-start(bf16[128,1536]{1,0:T(8,128)(2,1)S(1)} %pad_maximum_fusion.1), channel_id=1, source_target_pairs={{0,16},{16,32},{32,48},{48,0},{1,17},{17,33},{33,49},{49,1},{2,18}... | collective-permute-start | bytes 1179656 | tf_op jit(solution)/shard_map/ppermute | solution.py:22
  162.6 21.5 %collective-permute-start.37 = (bf16[128,1536]{1,0:T(8,128)(2,1)S(1)}, bf16[128,1536]{1,0:T(8,128)(2,1)S(1)}, u32[]{:S(2)}, u32[]{:S(2)}) collective-permute-start(bf16[128,1536]{1,0:T(8,128)(2,1)S(1)} %pad_maximum_fusion.2), channel_id=1, source_target_pairs={{0,48},{16,0},{32,16},{48,32},{1,49},{17,1},{33,17},{49,33},{2,50}... | collective-permute-start | bytes 1179656 | tf_op jit(solution)/shard_map/ppermute | solution.py:22
  165.4 11.8 %collective-permute-start.43 = (bf16[512,256]{1,0:T(8,128)(2,1)S(1)}, bf16[512,256]{1,0:T(8,128)(2,1)S(1)}, u32[]{:S(2)}, u32[]{:S(2)}) collective-permute-start(bf16[512,256]{1,0:T(8,128)(2,1)S(1)} %collective-permute-done.33), channel_id=1, source_target_pairs={{0,1},{1,0},{2,3},{3,2},{4,5},{5,4},{6,7},{7,6},{8,9},{9,8},{10,11... | collective-permute-start | bytes 786440 | tf_op jit(solution)/shard_map/ppermute | solution.py:22
  168.7 8.0 %collective-permute-start.42 = (bf16[512,256]{1,0:T(8,128)(2,1)S(1)}, bf16[512,256]{1,0:T(8,128)(2,1)S(1)}, u32[]{:S(2)}, u32[]{:S(2)}) collective-permute-start(bf16[512,256]{1,0:T(8,128)(2,1)S(1)} %collective-permute-done.41), channel_id=1, source_target_pairs={{0,6},{2,0},{4,2},{6,4},{1,7},{3,1},{5,3},{7,5},{8,14},{10,8},{12,... | collective-permute-start | bytes 786440 | tf_op jit(solution)/shard_map/ppermute | solution.py:22
  170.0 7.6 %collective-permute-start.44 = (bf16[512,256]{1,0:T(8,128)(2,1)S(1)}, bf16[512,256]{1,0:T(8,128)(2,1)S(1)}, u32[]{:S(2)}, u32[]{:S(2)}) collective-permute-start(bf16[512,256]{1,0:T(8,128)(2,1)S(1)} %collective-permute-done.41), channel_id=1, source_target_pairs={{0,2},{2,4},{4,6},{6,0},{1,3},{3,5},{5,7},{7,1},{8,10},{10,12},{12... | collective-permute-start | bytes 786440 | tf_op jit(solution)/shard_map/ppermute | solution.py:22
  176.8 21.3 %collective-permute-start.39 = (bf16[64,1536]{1,0:T(8,128)(2,1)S(1)}, bf16[64,1536]{1,0:T(8,128)(2,1)S(1)}, u32[]{:S(2)}, u32[]{:S(2)}) collective-permute-start(bf16[64,1536]{1,0:T(8,128)(2,1)S(1)} %fusion.54), channel_id=1, source_target_pairs={{0,32},{16,48},{32,0},{48,16},{1,33},{17,49},{33,1},{49,17},{2,34}... | collective-permute-start | bytes 589832 | tf_op jit(solution)/shard_map/ppermute | solution.py:22
  179.5 6.8 %collective-permute-start.47 = (bf16[64,1536]{1,0:T(8,128)(2,1)S(1)}, bf16[64,1536]{1,0:T(8,128)(2,1)S(1)}, u32[]{:S(2)}, u32[]{:S(2)}) collective-permute-start(bf16[64,1536]{1,0:T(8,128)(2,1)S(1)} %get-tuple-element.30), channel_id=1, source_target_pairs={{0,64},{64,0},{1,65},{65,1},{2,66},{66,2},{3,67},{67,3},{4,68},{68... | collective-permute-start | bytes 589832 | tf_op jit(solution)/shard_map/ppermute | solution.py:22
  180.6 16.1 %collective-permute-start.45 = (bf16[128,1536]{1,0:T(8,128)(2,1)S(1)}, bf16[128,1536]{1,0:T(8,128)(2,1)S(1)}, u32[]{:S(2)}, u32[]{:S(2)}) collective-permute-start(bf16[128,1536]{1,0:T(8,128)(2,1)S(1)} %pad_maximum_fusion.3), channel_id=1, source_target_pairs={{0,16},{16,32},{32,48},{48,0},{1,17},{17,33},{33,49},{49,1},{2,18}... | collective-permute-start | bytes 1179656 | tf_op jit(solution)/shard_map/ppermute | solution.py:22
  181.1 15.7 %collective-permute-start.46 = (bf16[128,1536]{1,0:T(8,128)(2,1)S(1)}, bf16[128,1536]{1,0:T(8,128)(2,1)S(1)}, u32[]{:S(2)}, u32[]{:S(2)}) collective-permute-start(bf16[128,1536]{1,0:T(8,128)(2,1)S(1)} %pad_maximum_fusion.4), channel_id=1, source_target_pairs={{0,48},{16,0},{32,16},{48,32},{1,49},{17,1},{33,17},{49,33},{2,50}... | collective-permute-start | bytes 1179656 | tf_op jit(solution)/shard_map/ppermute | solution.py:22
  184.3 13.8 %collective-permute-start.40 = (bf16[64,1536]{1,0:T(8,128)(2,1)S(1)}, bf16[64,1536]{1,0:T(8,128)(2,1)S(1)}, u32[]{:S(2)}, u32[]{:S(2)}) collective-permute-start(bf16[64,1536]{1,0:T(8,128)(2,1)S(1)} %fusion.53), channel_id=1, source_target_pairs={{0,64},{64,0},{1,65},{65,1},{2,66},{66,2},{3,67},{67,3},{4,68},{68... | collective-permute-start | bytes 589832 | tf_op jit(solution)/shard_map/ppermute | solution.py:22
  186.4 11.8 %collective-permute-start.48 = (bf16[64,1536]{1,0:T(8,128)(2,1)S(1)}, bf16[64,1536]{1,0:T(8,128)(2,1)S(1)}, u32[]{:S(2)}, u32[]{:S(2)}) collective-permute-start(bf16[64,1536]{1,0:T(8,128)(2,1)S(1)} %fusion.50), channel_id=1, source_target_pairs={{0,32},{16,48},{32,0},{48,16},{1,33},{17,49},{33,1},{49,17},{2,34}... | collective-permute-start | bytes 589832 | tf_op jit(solution)/shard_map/ppermute | solution.py:22
  (11 other events, 92.2 us)
